TPU v7x, 8 devices: a whole 2x2x1 slice. The times are simulated.
8 devices in a mesh: dp: 4 (over z, y, x), sp: 2 (over core).
Axes of the slice: x: 2, y: 2, z: 1, core: 2. Of those that a mesh axis runs over, the one named last changes fastest.
Arguments:
- act_in: bfloat16 [4, 4096, 1536], P('dp', 'sp')
- positions: int32 [4, 4096], P('dp', 'sp')
- out_grad: bfloat16 [4, 4096, 1536], P('dp', 'sp')
- norm1_gain: bfloat16 [1536], P(('dp', 'sp'))
- norm2_gain: bfloat16 [1536], P(('dp', 'sp'))
- w_query: bfloat16 [1536, 12, 128], P(('dp', 'sp'))
- w_key: bfloat16 [1536, 2, 128], P(('dp', 'sp'))
- w_value: bfloat16 [1536, 2, 128], P(('dp', 'sp'))
- w_out: bfloat16 [1536, 1536], P(('dp', 'sp'))
- w_gate: bfloat16 [1536, 8960], P(('dp', 'sp'))
- w_up: bfloat16 [1536, 8960], P(('dp', 'sp'))
- w_down: bfloat16 [8960, 1536], P(('dp', 'sp'))
Outputs:
- output 1: bfloat16 [4, 4096, 1536], P('dp', 'sp')
- output 2: bfloat16 [4, 4096, 1536], P('dp', 'sp')
- output 3: float32 [1536], P(('dp', 'sp'))
- output 4: float32 [1536], P(('dp', 'sp'))
- output 5: float32 [1536, 12, 128], P(('dp', 'sp'))
- output 6: float32 [1536, 2, 128], P(('dp', 'sp'))
- output 7: float32 [1536, 2, 128], P(('dp', 'sp'))
- output 8: float32 [1536, 1536], P(('dp', 'sp'))
- output 9: float32 [1536, 8960], P(('dp', 'sp'))
- output 10: float32 [1536, 8960], P(('dp', 'sp'))
- output 11: float32 [8960, 1536], P(('dp', 'sp'))
All inputs are finite; a program needn't handle non-finite values.
Results may differ from a plain program's by a relative error of at most 0.0153044.
Values are sent between devices in bfloat16 or wider.
A program may use at most 1 GiB of HBM per device.

v0:
```python
import math
import jax
import jax.numpy as jnp
from jax import lax
from jax.sharding import PartitionSpec as P

EPS = 1e-5
ROPE_BASE = 10000.0
NEG_BIG = -1e30


def rms_forward(rows_f32, gain_vec):
    row_scale = lax.rsqrt(jnp.mean(rows_f32 * rows_f32, axis=-1, keepdims=True) + EPS)
    unit_rows = rows_f32 * row_scale
    return (unit_rows * gain_vec.astype(jnp.float32)).astype(jnp.bfloat16), unit_rows, row_scale


def rms_backward(grad_normed, unit_rows, row_scale, gain_vec):
    gain_grad = jnp.sum(grad_normed * unit_rows, axis=(0, 1))
    grad_unit = grad_normed * gain_vec.astype(jnp.float32)
    inner_mean = jnp.mean(grad_unit * unit_rows, axis=-1, keepdims=True)
    return row_scale * (grad_unit - unit_rows * inner_mean), gain_grad


def rope_tables(positions, head_dim):
    half_dim = head_dim // 2
    inv_freq = ROPE_BASE ** (-(jnp.arange(half_dim, dtype=jnp.float32) * (2.0 / head_dim)))
    angles = positions.astype(jnp.float32)[..., None] * inv_freq
    return jnp.cos(angles)[..., None, :], jnp.sin(angles)[..., None, :]


def rope_apply(values, cos_t, sin_t, rot_sign):
    half_dim = values.shape[-1] // 2
    first_half = values[..., :half_dim]
    second_half = values[..., half_dim:]
    return jnp.concatenate([first_half * cos_t - rot_sign * second_half * sin_t, second_half * cos_t + rot_sign * first_half * sin_t], axis=-1)


def attn_forward(q_rot, k_rot, v_proj, q_offset, q_block):
    n_batch, q_len, n_heads, head_dim = q_rot.shape
    k_len, n_kv = k_rot.shape[1], k_rot.shape[2]
    n_group = n_heads // n_kv
    attn_scale = head_dim ** -0.5
    key_index = jnp.arange(k_len)

    def block_step(block_idx, loop_state):
        out_buf, norm_buf = loop_state
        q_start = block_idx * q_block
        q_blk = lax.dynamic_slice_in_dim(q_rot, q_start, q_block, axis=1).reshape(n_batch, q_block, n_kv, n_group, head_dim)
        scores = jnp.einsum("bqkgd,bskd->bkgqs", q_blk, k_rot, preferred_element_type=jnp.float32) * attn_scale
        allowed = (q_offset + q_start + jnp.arange(q_block))[:, None] >= key_index[None, :]
        scores = jnp.where(allowed, scores, NEG_BIG)
        row_max = jnp.max(scores, axis=-1, keepdims=True)
        exp_scores = jnp.exp(scores - row_max)
        row_sum = jnp.sum(exp_scores, axis=-1, keepdims=True)
        prob_bf = (exp_scores / row_sum).astype(jnp.bfloat16)
        out_blk = jnp.einsum("bkgqs,bskd->bqkgd", prob_bf, v_proj, preferred_element_type=jnp.float32)
        out_blk = out_blk.astype(jnp.bfloat16).reshape(n_batch, q_block, n_heads, head_dim)
        norm_blk = (row_max + jnp.log(row_sum))[..., 0]
        out_buf = lax.dynamic_update_slice_in_dim(out_buf, out_blk, q_start, axis=1)
        norm_buf = lax.dynamic_update_slice_in_dim(norm_buf, norm_blk, q_start, axis=3)
        return out_buf, norm_buf

    init_state = (jnp.zeros(q_rot.shape, jnp.bfloat16), jnp.zeros((n_batch, n_kv, n_group, q_len), jnp.float32))
    return lax.fori_loop(0, q_len // q_block, block_step, init_state)


def attn_backward(q_rot, k_rot, v_proj, grad_out, log_norm, q_offset, q_block):
    n_batch, q_len, n_heads, head_dim = q_rot.shape
    k_len, n_kv = k_rot.shape[1], k_rot.shape[2]
    n_group = n_heads // n_kv
    attn_scale = head_dim ** -0.5
    key_index = jnp.arange(k_len)

    def block_step(block_idx, loop_state):
        dq_buf, dk_acc, dv_acc = loop_state
        q_start = block_idx * q_block
        q_blk = lax.dynamic_slice_in_dim(q_rot, q_start, q_block, axis=1).reshape(n_batch, q_block, n_kv, n_group, head_dim)
        do_blk = lax.dynamic_slice_in_dim(grad_out, q_start, q_block, axis=1).reshape(n_batch, q_block, n_kv, n_group, head_dim)
        norm_blk = lax.dynamic_slice_in_dim(log_norm, q_start, q_block, axis=3)
        scores = jnp.einsum("bqkgd,bskd->bkgqs", q_blk, k_rot, preferred_element_type=jnp.float32) * attn_scale
        allowed = (q_offset + q_start + jnp.arange(q_block))[:, None] >= key_index[None, :]
        scores = jnp.where(allowed, scores, NEG_BIG)
        probs_f = jnp.exp(scores - norm_blk[..., None])
        grad_prob = jnp.einsum("bqkgd,bskd->bkgqs", do_blk, v_proj, preferred_element_type=jnp.float32)
        grad_scores = probs_f * (grad_prob - jnp.sum(probs_f * grad_prob, axis=-1, keepdims=True))
        grad_scores = (grad_scores * attn_scale).astype(jnp.bfloat16)
        dq_blk = jnp.einsum("bkgqs,bskd->bqkgd", grad_scores, k_rot, preferred_element_type=jnp.float32)
        dq_blk = dq_blk.astype(jnp.bfloat16).reshape(n_batch, q_block, n_heads, head_dim)
        dk_acc = dk_acc + jnp.einsum("bkgqs,bqkgd->bskd", grad_scores, q_blk, preferred_element_type=jnp.float32)
        dv_acc = dv_acc + jnp.einsum("bkgqs,bqkgd->bskd", probs_f.astype(jnp.bfloat16), do_blk, preferred_element_type=jnp.float32)
        dq_buf = lax.dynamic_update_slice_in_dim(dq_buf, dq_blk, q_start, axis=1)
        return dq_buf, dk_acc, dv_acc

    init_state = (jnp.zeros(q_rot.shape, jnp.bfloat16), jnp.zeros(k_rot.shape, jnp.float32), jnp.zeros(v_proj.shape, jnp.float32))
    return lax.fori_loop(0, q_len // q_block, block_step, init_state)


def solution(mesh):
    flat_axes = ("dp", "sp")
    row_spec = P("dp", "sp", None)
    pos_spec = P("dp", "sp")
    vec_spec = P(flat_axes)
    mat_spec = P(flat_axes, None)
    cube_spec = P(flat_axes, None, None)

    def gather(local_part):
        return lax.all_gather(local_part, flat_axes, axis=0, tiled=True)

    def scatter_sum(full_arr):
        return lax.psum_scatter(full_arr, flat_axes, scatter_dimension=0, tiled=True)

    def to_heads(values):
        return lax.all_to_all(values, "sp", 2, 1, tiled=True)

    def to_tokens(values):
        return lax.all_to_all(values, "sp", 1, 2, tiled=True)

    def local_step(act_in, positions, out_grad, norm1_gain, norm2_gain, w_query, w_key, w_value, w_out, w_gate, w_up, w_down):
        full_gain1 = gather(norm1_gain)
        full_gain2 = gather(norm2_gain)
        full_query = gather(w_query)
        full_key = gather(w_key)
        full_value = gather(w_value)
        full_out = gather(w_out)
        full_gate = gather(w_gate)
        full_up = gather(w_up)
        full_down = gather(w_down)
        act_f = act_in.astype(jnp.float32)
        normed_a, unit_a, scale_a = rms_forward(act_f, full_gain1)
        cos_t, sin_t = rope_tables(positions, w_query.shape[2])
        q_rot = rope_apply(jnp.einsum("btd,dhe->bthe", normed_a, full_query, preferred_element_type=jnp.float32), cos_t, sin_t, 1.0).astype(jnp.bfloat16)
        k_rot = rope_apply(jnp.einsum("btd,dhe->bthe", normed_a, full_key, preferred_element_type=jnp.float32), cos_t, sin_t, 1.0).astype(jnp.bfloat16)
        v_proj = jnp.einsum("btd,dhe->bthe", normed_a, full_value, preferred_element_type=jnp.float32).astype(jnp.bfloat16)
        q_heads = to_heads(q_rot)
        k_heads = to_heads(k_rot)
        v_heads = to_heads(v_proj)
        q_block = math.gcd(q_heads.shape[1], 256)
        attn_heads, log_norm = attn_forward(q_heads, k_heads, v_heads, 0, q_block)
        attn_seq = to_tokens(attn_heads)
        attn_flat = attn_seq.reshape(attn_seq.shape[0], attn_seq.shape[1], -1)
        hidden = (act_f + jnp.einsum("btf,fd->btd", attn_flat, full_out, preferred_element_type=jnp.float32)).astype(jnp.bfloat16)
        hidden_f = hidden.astype(jnp.float32)
        normed_b, unit_b, scale_b = rms_forward(hidden_f, full_gain2)
        gate_pre = jnp.einsum("btd,df->btf", normed_b, full_gate, preferred_element_type=jnp.float32)
        up_pre = jnp.einsum("btd,df->btf", normed_b, full_up, preferred_element_type=jnp.float32)
        gate_sig = jax.nn.sigmoid(gate_pre)
        gate_act = gate_pre * gate_sig
        mixed_act = (gate_act * up_pre).astype(jnp.bfloat16)
        act_out = (hidden_f + jnp.einsum("btf,fd->btd", mixed_act, full_down, preferred_element_type=jnp.float32)).astype(jnp.bfloat16)

        back_gain1 = gather(norm1_gain)
        back_gain2 = gather(norm2_gain)
        back_query = gather(w_query)
        back_key = gather(w_key)
        back_value = gather(w_value)
        back_out = gather(w_out)
        back_gate = gather(w_gate)
        back_up = gather(w_up)
        back_down = gather(w_down)
        grad_mixed = jnp.einsum("btd,fd->btf", out_grad, back_down, preferred_element_type=jnp.float32).astype(jnp.bfloat16).astype(jnp.float32)
        down_grad = jnp.einsum("btf,btd->fd", mixed_act, out_grad, preferred_element_type=jnp.float32)
        grad_up = (grad_mixed * gate_act).astype(jnp.bfloat16)
        grad_gate = (grad_mixed * up_pre * gate_sig * (1.0 + gate_pre * (1.0 - gate_sig))).astype(jnp.bfloat16)
        gate_grad = jnp.einsum("btd,btf->df", normed_b, grad_gate, preferred_element_type=jnp.float32)
        up_grad = jnp.einsum("btd,btf->df", normed_b, grad_up, preferred_element_type=jnp.float32)
        grad_normed_b = (jnp.einsum("btf,df->btd", grad_gate, back_gate, preferred_element_type=jnp.float32) + jnp.einsum("btf,df->btd", grad_up, back_up, preferred_element_type=jnp.float32)).astype(jnp.bfloat16).astype(jnp.float32)
        grad_rows_b, gain2_grad = rms_backward(grad_normed_b, unit_b, scale_b, back_gain2)
        grad_hidden = (out_grad.astype(jnp.float32) + grad_rows_b).astype(jnp.bfloat16)
        wout_grad = jnp.einsum("btf,btd->fd", attn_flat, grad_hidden, preferred_element_type=jnp.float32)
        grad_attn = jnp.einsum("btd,fd->btf", grad_hidden, back_out, preferred_element_type=jnp.float32).astype(jnp.bfloat16).reshape(attn_seq.shape)
        grad_attn_heads = to_heads(grad_attn)
        dq_heads, dk_heads, dv_heads = attn_backward(q_heads, k_heads, v_heads, grad_attn_heads, log_norm, 0, q_block)
        dq_seq = to_tokens(dq_heads)
        dk_seq = to_tokens(dk_heads.astype(jnp.bfloat16))
        dv_seq = to_tokens(dv_heads.astype(jnp.bfloat16))
        grad_q = rope_apply(dq_seq.astype(jnp.float32), cos_t, sin_t, -1.0).astype(jnp.bfloat16)
        grad_k = rope_apply(dk_seq.astype(jnp.float32), cos_t, sin_t, -1.0).astype(jnp.bfloat16)
        query_grad = jnp.einsum("btd,bthe->dhe", normed_a, grad_q, preferred_element_type=jnp.float32)
        key_grad = jnp.einsum("btd,bthe->dhe", normed_a, grad_k, preferred_element_type=jnp.float32)
        value_grad = jnp.einsum("btd,bthe->dhe", normed_a, dv_seq, preferred_element_type=jnp.float32)
        grad_normed_a = (jnp.einsum("bthe,dhe->btd", grad_q, back_query, preferred_element_type=jnp.float32) + jnp.einsum("bthe,dhe->btd", grad_k, back_key, preferred_element_type=jnp.float32) + jnp.einsum("bthe,dhe->btd", dv_seq, back_value, preferred_element_type=jnp.float32)).astype(jnp.bfloat16).astype(jnp.float32)
        grad_rows_a, gain1_grad = rms_backward(grad_normed_a, unit_a, scale_a, back_gain1)
        in_grad = (grad_hidden.astype(jnp.float32) + grad_rows_a).astype(jnp.bfloat16)
        return (act_out, in_grad, scatter_sum(gain1_grad), scatter_sum(gain2_grad), scatter_sum(query_grad), scatter_sum(key_grad), scatter_sum(value_grad), scatter_sum(wout_grad), scatter_sum(gate_grad), scatter_sum(up_grad), scatter_sum(down_grad))

    return jax.shard_map(local_step, mesh=mesh, in_specs=(row_spec, pos_spec, row_spec, vec_spec, vec_spec, cube_spec, cube_spec, cube_spec, mat_spec, mat_spec, mat_spec, mat_spec), out_specs=(row_spec, row_spec, vec_spec, vec_spec, cube_spec, cube_spec, cube_spec, mat_spec, mat_spec, mat_spec, mat_spec), check_vma=False)
```

profile of v0, /device:TPU:0, one launch (start us, length us, event | category | flops | bytes accessed | tf_op | source)
XLA Modules:
  0.0 3723.9 jit_solution(9845794070710271255)
XLA Ops:
  19.2 26.2 all-reduce.5
  45.5 17.9 all_gather.38
  163.7 600.7 %while.34 = (s32[]{:T(128)}, bf16[1,4096,6,128]{3,1,2,0:T(8,128)(2,1)}, f32[1,1,6,4096]{3,2,1,0:T(8,128)S(1)}, bf16[1,4096,6,128]{3,1,2,0:T(8,128)(2,1)}, bf16[1...) while((s32[]{:T(128)}, ...), condition=%wide.region_4.5_spmd.clone, body=%wide.region_1.4_spmd.clone.sunk | while | flops 3297966848 | bytes 82632856 | solution.py:65
  264.7 16.7 fusion.192
  795.0 17.1 fusion.96
  812.2 65.3 %convolution_convert_fusion.1 = bf16[2048,8960]{1,0:T(8,128)(2,1)} fusion(bf16[8960,1536]{1,0:T(8,128)(2,1)} %all-gather.14.cloned.1.call-done, bf16[1,2048,1536]{2,1,0:T(8,128)(2,1)} %param.18), kind=kOutput, calls=%fused_computation.75 | convolution fusion | flops 56389795840 | bytes 70516736 | tf_op jit(solution)/shard_map/btd,fd->btf/dot_general | solution.py:161
  877.4 70.3 %fusion.125 = f32[2048,8960]{1,0:T(8,128)} fusion(bf16[1536,8960]{1,0:T(8,128)(2,1)} %all-gather.10.cloned.1.call-done, bf16[1,2048,1536]{1,2,0:T(8,128)(2,1)} %get-tuple-element.470, f32[1536]{0:T(1024)S(1)} %copy-done.32, f32[2048]{0:T(1024)S(1)} %add_rsqrt_fusion), kind=kOutput, calls=%fused_computation.165 | convolution fusion | flops 56384028672 | bytes 107231232 | tf_op jit(solution)/shard_map/btd,df->btf/dot_general | solution.py:145
  947.8 109.8 %fusion.67 = (bf16[2048,8960]{1,0:T(8,128)(2,1)}, bf16[2048,8960]{1,0:T(8,128)(2,1)}, bf16[2048,8960]{1,0:T(8,128)(2,1)}) fusion(bf16[2048,8960]{1,0:T(8,128)(2,1)} %convolution_convert_fusion.1, f32[2048,8960]{1,0:T(8,128)} %fusion.125, bf16[1536,8960]{1,0:T(8,128)(2,1)} %all-gather.12.cloned.1.call-done, bf16[1,2048,1536]{1,2,0:T(8,128)(2,1)} %get-tuple-element.470, ...), kind=kOutput, calls=%fused_computation.70 | convolution fusion | flops 56677629952 | bytes 254031872 | tf_op jit(solution)/shard_map/btd,df->btf/dot_general | solution.py:146
  1057.5 67.9 %fusion.127 = f32[2048,1536]{0,1:T(8,128)} fusion(bf16[2048,8960]{1,0:T(8,128)(2,1)} %get-tuple-element.455, bf16[1536,8960]{1,0:T(8,128)(2,1)} %all-gather.10.cloned.1.call-done), kind=kOutput, calls=%fused_computation.166 | convolution fusion | flops 56371445760 | bytes 76808192 | tf_op jit(solution)/shard_map/btf,df->btd/dot_general | solution.py:167
  1125.4 77.5 %fusion.95 = (f32[1536]{0:T(1024)}, f32[2048]{0:T(1024)S(1)}, bf16[2048,1536]{0,1:T(8,128)(2,1)}) fusion(bf16[1,2048,1536]{1,2,0:T(8,128)(2,1)} %get-tuple-element.470, f32[2048]{0:T(1024)S(1)} %add_rsqrt_fusion, f32[1536]{0:T(1024)S(1)} %copy-done.32, f32[2048,1536]{0,1:T(8,128)} %fusion.127, bf16[2048,8960]{1,0:T(8,128)(2,1)} %get-tuple-element.457, ...), kind=kOutput, calls=%fused_computation.111 | convolution fusion | flops 56402903040 | bytes 89419776 | tf_op jit(solution)/shard_map/btf,df->btd/dot_general | solution.py:167
  1245.2 1236.4 %while.35 = (s32[]{:T(128)}, bf16[1,4096,6,128]{3,1,2,0:T(8,128)(2,1)}, f32[1,4096,1,128]{1,3,2,0:T(8,128)}, f32[1,4096,1,128]{1,3,2,0:T(8,128)}, bf16[1,4096,6,...) while((s32[]{:T(128)}, ...), condition=%wide.region_9.0_spmd.clone, body=%wide.region_7.0_spmd.clone.sunk | while | flops 8157068288 | bytes 256815344 | solution.py:96
  1274.4 17.8 fusion.203
  1350.6 17.8 fusion.203
  1411.3 16.6 fusion.202
  1427.9 17.8 fusion.203
  1488.6 16.6 fusion.202
  1505.2 17.8 fusion.203
  1565.9 16.6 fusion.202
  1582.5 17.8 fusion.203
  1659.8 17.8 fusion.203
  1720.6 16.6 fusion.202
  1737.2 17.8 fusion.203
  1797.9 16.6 fusion.202
  1814.5 17.8 fusion.203
  1875.2 16.6 fusion.202
  1891.8 17.8 fusion.203
  1969.1 17.8 fusion.203
  2029.8 16.6 fusion.202
  2046.4 17.8 fusion.203
  2107.2 16.6 fusion.202
  2123.7 17.8 fusion.203
  2184.5 16.6 fusion.202
  2201.0 17.8 fusion.203
  2261.8 16.6 fusion.202
  2278.3 17.8 fusion.203
  2339.1 16.6 fusion.202
  2355.7 17.8 fusion.203
  2433.0 17.8 fusion.203
  2489.9 23.4 reduce.14
  2572.0 23.4 reduce.13
  2649.5 69.2 %fusion.121 = f32[1536,8960]{1,0:T(8,128)} fusion(bf16[2048,8960]{1,0:T(8,128)(2,1)} %get-tuple-element.455, bf16[1,2048,1536]{1,2,0:T(8,128)(2,1)} %get-tuple-element.470, f32[1536]{0:T(1024)S(1)} %copy-done.33, f32[2048]{0:T(1024)S(1)} %copy-done.35), kind=kOutput, calls=%fused_computation.163 | convolution fusion | flops 56384028672 | bytes 98056192 | tf_op jit(solution)/shard_map/btd,btf->df/dot_general | solution.py:165
  2718.9 68.3 %fusion.119 = f32[1536,8960]{1,0:T(8,128)} fusion(bf16[2048,8960]{1,0:T(8,128)(2,1)} %get-tuple-element.457, bf16[1,2048,1536]{1,2,0:T(8,128)(2,1)} %get-tuple-element.470, f32[1536]{0:T(1024)S(1)} %copy-done.33, f32[2048]{0:T(1024)S(1)} %copy-done.35), kind=kOutput, calls=%fused_computation.162 | convolution fusion | flops 56384028672 | bytes 98056192 | tf_op jit(solution)/shard_map/btd,btf->df/dot_general | solution.py:166
  2787.2 67.7 %fusion.104 = f32[8960,1536]{1,0:T(8,128)} fusion(bf16[2048,8960]{1,0:T(8,128)(2,1)} %get-tuple-element.456, bf16[1,2048,1536]{2,1,0:T(8,128)(2,1)} %param.18), kind=kOutput, calls=%fused_computation.126 | convolution fusion | flops 56371445760 | bytes 98041856 | tf_op jit(solution)/shard_map/btf,btd->fd/dot_general | solution.py:162
  2893.3 23.5 all-reduce.4
  2939.4 67.0 %fusion.97 = bf16[1,2048,1536]{1,2,0:T(8,128)(2,1)} fusion(bf16[1,2048,1536]{1,2,0:T(8,128)(2,1)} %get-tuple-element.470, bf16[2048,8960]{1,0:T(8,128)(2,1)} %get-tuple-element.456, bf16[8960,1536]{1,0:T(8,128)(2,1)} %all-gather.14.cloned.1.call-done), kind=kOutput, calls=%fused_computation.113 | convolution fusion | flops 56380882944 | bytes 76808192 | tf_op jit(solution)/shard_map/btf,fd->btd/dot_general | solution.py:150
  3018.6 79.0 %reduce-scatter.16.cloned.1.call-done = f32[192,8960]{1,0:T(8,128)} async-done(((f32[1536,8960]{1,0:T(8,128)}), f32[192,8960]{1,0:T(8,128)}) %reduce-scatter.16.cloned.1.call-update) | async-done | bytes 6881296 | tf_op jit(solution)/shard_map/reduce_scatter | solution.py:111
  3097.6 309.7 %reduce-scatter.18.cloned.1.call-done = f32[192,8960]{1,0:T(8,128)} async-done(((f32[1536,8960]{1,0:T(8,128)}), f32[192,8960]{1,0:T(8,128)}) %reduce-scatter.18.cloned.1.call-update) | async-done | bytes 6881296 | tf_op jit(solution)/shard_map/reduce_scatter | solution.py:111
  3407.3 309.5 %reduce-scatter.20.cloned.1.call-done = f32[1120,1536]{1,0:T(8,128)} async-done(((f32[8960,1536]{1,0:T(8,128)}), f32[1120,1536]{1,0:T(8,128)}) %reduce-scatter.20.cloned.1.call-update) | async-done | bytes 6881296 | tf_op jit(solution)/shard_map/reduce_scatter | solution.py:111
  (442 shorter events, 1731.0 us)
Async XLA Ops:
  7.2 11.5 copy-start.39
  7.2 11.8 copy-start.40
  7.2 38.2 %copy-start.30 = (bf16[192,2,128]{2,1,0:T(2,128)(2,1)S(1)}, bf16[192,2,128]{2,1,0:T(2,128)(2,1)}, u32[]{:S(2)}) copy-start(bf16[192,2,128]{2,1,0:T(2,128)(2,1)} %param.22) | copy-start | bytes 294916
  7.2 38.3 %copy-start.36 = (s32[1,2048]{1,0:T(1,128)S(1)}, s32[1,2048]{1,0:T(1,128)}, u32[]{:S(2)}) copy-start(s32[1,2048]{1,0:T(1,128)} %param.17) | copy-start | bytes 24580
  7.2 105.6 %all-gather.6.cloned.1.call-start = ((), (), s32[]{:S(2)}) async-start(), calls=%async_computation.15 | async-start | bytes 5308416 | tf_op jit(solution)/shard_map/all_gather | solution.py:108
  8.0 787.0 %all-gather.8.cloned.1.call-start = ((), (), s32[]{:S(2)}) async-start(), calls=%async_computation.16 | async-start | bytes 5308416 | tf_op jit(solution)/shard_map/all_gather | solution.py:108
  8.7 803.5 %all-gather.14.cloned.1.call-start = ((), (), s32[]{:S(2)}) async-start(), calls=%async_computation.19 | async-start | bytes 30965760 | tf_op jit(solution)/shard_map/all_gather | solution.py:108
  9.4 868.0 %all-gather.10.cloned.1.call-start = ((), (), s32[]{:S(2)}) async-start(), calls=%async_computation.17 | async-start | bytes 30965760 | tf_op jit(solution)/shard_map/all_gather | solution.py:108
  45.4 25.1 copy-start.1
  45.4 31.2 copy-start.26
  63.4 13.2 copy-start.19
  67.8 8.8 copy-start.28
  70.5 56.4 %copy-start.7 = (f32[2048,64]{0,1:T(8,128)}, f32[2048,64]{0,1:T(8,128)S(1)}, u32[]{:S(2)}) copy-start(f32[2048,64]{0,1:T(8,128)S(1)} %get-tuple-element.468) | copy-start | bytes 1572868
  74.7 7.5 copy-start.31
  78.0 34.2 all-to-all-start.1
  81.6 866.2 %all-gather.12.cloned.1.call-start = ((), (), s32[]{:S(2)}) async-start(), calls=%async_computation.18 | async-start | bytes 30965760 | tf_op jit(solution)/shard_map/all_gather | solution.py:108
  147.7 12.4 all-to-all-start.2
  151.3 2863.8 %reduce-scatter.10.cloned.1.call-start = ((), (), s32[]{:S(2)}) async-start(), calls=%async_computation.21 | async-start | bytes 1769472 | tf_op jit(solution)/shard_map/reduce_scatter | solution.py:111
  764.4 18.4 copy-start.2
  764.4 18.4 copy-start.4
  764.4 18.4 copy-start.25
  812.1 390.7 %copy-start.34 = (f32[2048]{0:T(1024)}, f32[2048]{0:T(1024)S(1)}, u32[]{:S(2)}) copy-start(f32[2048]{0:T(1024)S(1)} %add_rsqrt_fusion) | copy-start | bytes 24580
  812.1 65.3 %copy-start.32 = (f32[1536]{0:T(1024)S(1)}, f32[1536]{0:T(1024)}, u32[]{:S(2)}) copy-start(f32[1536]{0:T(1024)} %convert_element_type.226) | copy-start | bytes 18436
  1202.8 9.7 copy-start.38
  1212.5 10.3 copy-start.6
  1232.9 12.3 copy-start.3
  1232.9 12.3 copy-start.5
  1292.2 4.5 copy-start
  2481.5 43.0 %copy-start.8 = (f32[2048,64]{0,1:T(8,128)S(1)}, f32[2048,64]{0,1:T(8,128)}, u32[]{:S(2)}) copy-start(f32[2048,64]{0,1:T(8,128)} %copy-done.7) | copy-start | bytes 1572868
  2481.5 43.0 %copy-start.10 = (f32[2048,64]{0,1:T(8,128)S(1)}, f32[2048,64]{0,1:T(8,128)}, u32[]{:S(2)}) copy-start(f32[2048,64]{0,1:T(8,128)} %get-tuple-element.466) | copy-start | bytes 1572868
  2531.1 485.7 %reduce-scatter.12.cloned.1.call-start = ((), (), s32[]{:S(2)}) async-start(), calls=%async_computation.22 | async-start | bytes 1769472 | tf_op jit(solution)/shard_map/reduce_scatter | solution.py:111
  2611.0 407.7 %reduce-scatter.8.cloned.1.call-start = ((), (), s32[]{:S(2)}) async-start(), calls=%async_computation.20 | async-start | bytes 10616832 | tf_op jit(solution)/shard_map/reduce_scatter | solution.py:111
  2633.5 16.0 copy-start.33
  2633.5 16.0 copy-start.35
  2633.5 385.1 %reduce-scatter.14.cloned.1.call-start = ((), (), s32[]{:S(2)}) async-start(), calls=%async_computation.23 | async-start | bytes 10616832 | tf_op jit(solution)/shard_map/reduce_scatter | solution.py:111
  2649.5 448.1 %reduce-scatter.16.cloned.1.call-start = ((), (), s32[]{:S(2)}) async-start(), calls=%async_computation.24 | async-start | bytes 61931520 | tf_op jit(solution)/shard_map/reduce_scatter | solution.py:111
  2718.8 688.5 %reduce-scatter.18.cloned.1.call-start = ((), (), s32[]{:S(2)}) async-start(), calls=%async_computation.25 | async-start | bytes 61931520 | tf_op jit(solution)/shard_map/reduce_scatter | solution.py:111
  2787.2 929.6 %reduce-scatter.20.cloned.1.call-start = ((), (), s32[]{:S(2)}) async-start(), calls=%async_computation.26 | async-start | bytes 61931520 | tf_op jit(solution)/shard_map/reduce_scatter | solution.py:111
  2856.5 8.3 copy-start.16
  2856.5 8.3 copy-start.18
  2856.5 22.6 slice-start
  2864.8 14.3 slice-start.1
  2864.8 14.3 copy-start.20
  2864.8 14.3 copy-start.22
  2864.8 14.3 copy-start.24
  2864.9 14.3 copy-start.27
  2864.9 14.3 copy-start.29
  2879.2 14.2 copy-start.37
  (24 other events, 81.6 us)
Sparse Core Ops, SparseCore 0:
  9.9 37.1 all-gather.5
  48.9 35.6 all-gather.7
  86.4 129.5 all-gather.13
  217.7 129.5 all-gather.9
  349.0 129.5 all-gather.11
  2531.2 30.6 reduce-scatter.9
  2611.1 30.6 reduce-scatter.11
  2645.8 68.2 reduce-scatter.7
  2718.1 68.4 reduce-scatter.13
  2790.6 306.9 reduce-scatter.15
  3101.7 305.5 reduce-scatter.17
  3411.3 305.5 reduce-scatter.19
where the time goes:
time: 3740 us; the launch traced here: 3720 us
  matrix products  2040 us (55%)
  waiting for transfers between devices  701 us (19%)
  other arithmetic  599 us (16%)
  local copies, waits for them, and re-layouts  219 us (6%)
  blocking collectives  139 us (4%)
    reduce_scatter x7, waiting for transfers between devices, scatter_sum(): lax.psum_scatter(full_arr, flat_axes, scatter_dimension=0, tiled=True)  698 us
    dot_general x32, matrix products, block_step(): jnp.einsum('bqkgd,bskd->bkgqs', q_blk, k_rot, preferred_element_type=jnp....  369 us
    another operation x19, other arithmetic  290 us
    dot_general x16, matrix products, block_step(): jnp.einsum('bqkgd,bskd->bkgqs', do_blk, v_proj, preferred_element_type=jn...  265 us
    dot_general x16, matrix products, block_step(): jnp.einsum('bkgqs,bqkgd->bskd', probs_f.astype(jnp.bfloat16), do_blk, pre...  212 us
    dot_general x16, matrix products, block_step(): jnp.einsum('bkgqs,bskd->bqkgd', prob_bf, v_proj, preferred_element_type=j...  203 us
    reduce_sum x16, other arithmetic, block_step(): row_sum = jnp.sum(exp_scores, axis=-1, keepdims=True)  195 us
    dot_general x16, matrix products, block_step(): jnp.einsum('bkgqs,bqkgd->bskd', grad_scores, q_blk, preferred_element_typ...  135 us
  transfers between devices with their start and end apart: 14, of which 3 were waited for; matrix products, arithmetic and copies ran while one was open for 34% of the time, Pallas kernels for 0%

commit v1 on v0

v1 whole, which is shorter than its diff:
```python
import jax
import jax.numpy as jnp
from jax import lax
from jax.experimental import pallas as pl
from jax.experimental.pallas import tpu as pltpu
from jax.sharding import PartitionSpec as P


EPS = 1e-5
ROPE_BASE = 10000.0
NEG_BIG = -1e30
LOG2E = 1.4426950408889634
F32 = jnp.float32
BF16 = jnp.bfloat16

HD = 128
VMEM_LIMIT = 60 * 1024 * 1024
NT = (((1,), (1,)), ((), ()))


def dot(a, b):
    return jnp.dot(a, b, preferred_element_type=F32)


def dot_nt(a, b):
    return lax.dot_general(a, b, NT, preferred_element_type=F32)


def cost(flops, nbytes, trans=0):
    return pl.CostEstimate(flops=int(flops), bytes_accessed=int(nbytes), transcendentals=int(trans))


def qkv_kernel(x_ref, g_ref, w_ref, cos_ref, sin_ref, out_ref, u_ref):
    x = x_ref[...].astype(F32)
    scale = lax.rsqrt(jnp.mean(x * x, axis=-1, keepdims=True) + EPS)
    u = (x * scale * g_ref[...]).astype(BF16)
    u_ref[...] = u
    cos = cos_ref[...]
    sin = sin_ref[...]
    cols = w_ref.shape[1]
    step = 512
    per_core = cols // 2
    for n in range(cols // step):
        a = dot(u, w_ref[:, n * step:(n + 1) * step])
        for h in range(step // HD):
            col = n * step + h * HD
            part = a[:, h * HD:(h + 1) * HD]
            if (col % per_core) < per_core - HD:
                part = part * cos + pltpu.roll(part, HD // 2, 1) * sin
            out_ref[:, col:col + HD] = part.astype(BF16)


def qkv_project(x, gain, w_qkv, cos, sin):
    rows, dim = x.shape
    cols = w_qkv.shape[1]
    bm = 512
    return pl.pallas_call(
        qkv_kernel,
        grid=(rows // bm,),
        in_specs=[
            pl.BlockSpec((bm, dim), lambda i: (i, 0)),
            pl.BlockSpec((1, dim), lambda i: (0, 0)),
            pl.BlockSpec((dim, cols), lambda i: (0, 0)),
            pl.BlockSpec((bm, HD), lambda i: (i, 0)),
            pl.BlockSpec((bm, HD), lambda i: (i, 0)),
        ],
        out_specs=[pl.BlockSpec((bm, cols), lambda i: (i, 0)), pl.BlockSpec((bm, dim), lambda i: (i, 0))],
        out_shape=[jax.ShapeDtypeStruct((rows, cols), BF16), jax.ShapeDtypeStruct((rows, dim), BF16)],
        compiler_params=pltpu.CompilerParams(vmem_limit_bytes=VMEM_LIMIT),
        cost_estimate=cost(2 * rows * dim * cols, 2 * (2 * rows * dim + dim * cols + rows * cols)),
        name="qkv_project",
    )(x, gain, w_qkv, cos, sin)


BQ = 256
BK = 512


def attn_fwd_kernel(c_ref, q_ref, k_ref, v_ref, o_ref, lse_ref, vt_ref, m_ref, l_ref, acc_ref):
    i = pl.program_id(0)
    seq = k_ref.shape[0]
    n_kb = seq // BK
    n_head = q_ref.shape[1] // HD
    coef = HD ** -0.5 * LOG2E
    shift = c_ref[0] * (n_kb // 2)

    def phys(j):
        return pl.multiple_of(lax.rem(j + shift, n_kb) * BK, BK)

    @pl.when(i == 0)
    def _():
        for j in range(n_kb):
            vt_ref[j] = v_ref[pl.ds(phys(j), BK), :].astype(F32).T.astype(BF16)

    m_ref[...] = jnp.full_like(m_ref, NEG_BIG)
    l_ref[...] = jnp.zeros_like(l_ref)
    acc_ref[...] = jnp.zeros_like(acc_ref)

    def block(j, masked):
        k_blk = k_ref[pl.ds(phys(j), BK), :]
        vt = vt_ref[j]
        if masked:
            keys = j * BK + lax.broadcasted_iota(jnp.int32, (BK, BQ), 0)
            queries = i * BQ + lax.broadcasted_iota(jnp.int32, (BK, BQ), 1)
            allowed = keys <= queries
        for h in range(n_head):
            t = dot_nt(k_blk, q_ref[:, h * HD:(h + 1) * HD]) * coef
            if masked:
                t = jnp.where(allowed, t, NEG_BIG)
            m_prev = m_ref[h]
            m_new = jnp.maximum(m_prev, jnp.max(t, axis=0, keepdims=True))
            p = jnp.exp2(t - m_new)
            alpha = jnp.exp2(m_prev - m_new)
            m_ref[h] = m_new
            l_ref[h] = l_ref[h] * alpha + jnp.sum(p, axis=0, keepdims=True)
            acc_ref[h] = acc_ref[h] * alpha + dot(vt, p.astype(BF16))

    last = (i * BQ) // BK

    def body(j, carry):
        block(j, False)
        return carry

    lax.fori_loop(0, last, body, 0)
    block(last, True)
    for h in range(n_head):
        total = l_ref[h]
        o_ref[:, h * HD:(h + 1) * HD] = (acc_ref[h] / total).T.astype(BF16)
        lse_ref[0, h:h + 1, :] = m_ref[h] + jnp.log2(total)
    lse_ref[0, n_head:, :] = jnp.zeros_like(lse_ref[0, n_head:, :])


def attn_forward(core, qkv):
    seq, width = qkv.shape
    qw = width - 2 * HD
    n_head = qw // HD
    n_q = seq // BQ

    def rows(i, c):
        return (lax.rem(i + c[0] * (n_q // 2), n_q), 0)

    pairs = seq * seq // 2 * n_head
    return pl.pallas_call(
        attn_fwd_kernel,
        grid_spec=pltpu.PrefetchScalarGridSpec(
            num_scalar_prefetch=1,
            grid=(n_q,),
            in_specs=[
                pl.BlockSpec((BQ, qw), rows),
                pl.BlockSpec((seq, HD), lambda i, c: (0, n_head)),
                pl.BlockSpec((seq, HD), lambda i, c: (0, n_head + 1)),
            ],
            out_specs=[pl.BlockSpec((BQ, qw), rows), pl.BlockSpec((1, 8, BQ), lambda i, c: (i, 0, 0))],
            scratch_shapes=[
                pltpu.VMEM((seq // BK, HD, BK), BF16),
                pltpu.VMEM((n_head, 1, BQ), F32),
                pltpu.VMEM((n_head, 1, BQ), F32),
                pltpu.VMEM((n_head, HD, BQ), F32),
            ],
        ),
        out_shape=[jax.ShapeDtypeStruct((seq, qw), BF16), jax.ShapeDtypeStruct((n_q, 8, BQ), F32)],
        compiler_params=pltpu.CompilerParams(vmem_limit_bytes=VMEM_LIMIT),
        cost_estimate=cost(8 * pairs * HD, 4 * seq * width, pairs),
        name="attn_forward",
    )(core, qkv, qkv, qkv)


def attn_bwd_kernel(c_ref, q_ref, do_ref, o_ref, lse_ref, cos_ref, sin_ref, k_ref, v_ref, cos_all_ref, sin_all_ref,
                    dq_ref, dkv_ref, kt_ref, dqt_ref, delta_ref, dk_ref, dv_ref):
    i = pl.program_id(0)
    seq = k_ref.shape[0]
    n_kb = seq // BK
    n_head = q_ref.shape[1] // HD
    attn_scale = HD ** -0.5
    coef = attn_scale * LOG2E
    shift = c_ref[0] * (n_kb // 2)

    def phys(j):
        return pl.multiple_of(lax.rem(j + shift, n_kb) * BK, BK)

    @pl.when(i == 0)
    def _():
        for j in range(n_kb):
            kt_ref[j] = k_ref[pl.ds(phys(j), BK), :].astype(F32).T.astype(BF16)
        dk_ref[...] = jnp.zeros_like(dk_ref)
        dv_ref[...] = jnp.zeros_like(dv_ref)

    dqt_ref[...] = jnp.zeros_like(dqt_ref)
    for h in range(n_head):
        cols = slice(h * HD, (h + 1) * HD)
        prod = do_ref[:, cols].astype(F32) * o_ref[:, cols].astype(F32)
        delta_ref[h] = jnp.sum(prod.T, axis=0, keepdims=True)

    def block(j, masked):
        k_blk = k_ref[pl.ds(phys(j), BK), :]
        v_blk = v_ref[pl.ds(phys(j), BK), :]
        kt = kt_ref[j]
        dk = dk_ref[j]
        dv = dv_ref[j]
        if masked:
            keys = j * BK + lax.broadcasted_iota(jnp.int32, (BK, BQ), 0)
            queries = i * BQ + lax.broadcasted_iota(jnp.int32, (BK, BQ), 1)
            allowed = keys <= queries
        for h in range(n_head):
            cols = slice(h * HD, (h + 1) * HD)
            q_h = q_ref[:, cols]
            do_h = do_ref[:, cols]
            t = dot_nt(k_blk, q_h) * coef
            if masked:
                t = jnp.where(allowed, t, NEG_BIG)
            p = jnp.exp2(t - lse_ref[0, h:h + 1, :])
            ds = (p * (dot_nt(v_blk, do_h) - delta_ref[h])).astype(BF16)
            dv = dv + dot(p.astype(BF16), do_h)
            dk = dk + dot(ds, q_h)
            dqt_ref[h] = dqt_ref[h] + dot(kt, ds)
        dk_ref[j] = dk
        dv_ref[j] = dv

    last = (i * BQ) // BK

    def body(j, carry):
        block(j, False)
        return carry

    lax.fori_loop(0, last, body, 0)
    block(last, True)

    def unrotate(grad, cos, sin):
        grad = grad.astype(BF16).astype(F32)
        return (grad * cos - pltpu.roll(grad, HD // 2, 1) * sin).astype(BF16)

    for h in range(n_head):
        dq_ref[:, h * HD:(h + 1) * HD] = unrotate((dqt_ref[h] * attn_scale).T, cos_ref[...], sin_ref[...])

    @pl.when(i == pl.num_programs(0) - 1)
    def _():
        for j in range(n_kb):
            at = pl.ds(phys(j), BK)
            dkv_ref[at, :HD] = unrotate(dk_ref[j] * attn_scale, cos_all_ref[at, :], sin_all_ref[at, :])
            dkv_ref[at, HD:] = dv_ref[j].astype(BF16)


def attn_backward(core, qkv, grad_out, out, lse, cos, sin):
    seq, width = qkv.shape
    qw = width - 2 * HD
    n_head = qw // HD
    n_q = seq // BQ

    def rows(i, c):
        return (lax.rem(i + c[0] * (n_q // 2), n_q), 0)

    def whole(i, c):
        return (0, 0)

    pairs = seq * seq // 2 * n_head
    return pl.pallas_call(
        attn_bwd_kernel,
        grid_spec=pltpu.PrefetchScalarGridSpec(
            num_scalar_prefetch=1,
            grid=(n_q,),
            in_specs=[
                pl.BlockSpec((BQ, qw), rows),
                pl.BlockSpec((BQ, qw), rows),
                pl.BlockSpec((BQ, qw), rows),
                pl.BlockSpec((1, 8, BQ), lambda i, c: (i, 0, 0)),
                pl.BlockSpec((BQ, HD), rows),
                pl.BlockSpec((BQ, HD), rows),
                pl.BlockSpec((seq, HD), lambda i, c: (0, n_head)),
                pl.BlockSpec((seq, HD), lambda i, c: (0, n_head + 1)),
                pl.BlockSpec((seq, HD), whole),
                pl.BlockSpec((seq, HD), whole),
            ],
            out_specs=[pl.BlockSpec((BQ, qw), rows), pl.BlockSpec((seq, 2 * HD), whole)],
            scratch_shapes=[
                pltpu.VMEM((seq // BK, HD, BK), BF16),
                pltpu.VMEM((n_head, HD, BQ), F32),
                pltpu.VMEM((n_head, 1, BQ), F32),
                pltpu.VMEM((seq // BK, BK, HD), F32),
                pltpu.VMEM((seq // BK, BK, HD), F32),
            ],
        ),
        out_shape=[jax.ShapeDtypeStruct((seq, qw), BF16), jax.ShapeDtypeStruct((seq, 2 * HD), BF16)],
        compiler_params=pltpu.CompilerParams(vmem_limit_bytes=VMEM_LIMIT),
        cost_estimate=cost(20 * pairs * HD, 8 * seq * width, pairs),
        name="attn_backward",
    )(core, qkv, grad_out, out, lse, cos, sin, qkv, qkv, cos, sin)


FT = 640


def ffn_kernel(w_ref, dy_ref, w13_ref, w2_ref, mix_ref, dgu_ref):
    pre = dot(w_ref[...], w13_ref[...])
    dmix = dot_nt(dy_ref[...], w2_ref[...]).astype(BF16).astype(F32)
    gate = pre[:, :FT]
    up = pre[:, FT:]
    sig = jax.nn.sigmoid(gate)
    act = gate * sig
    mix_ref[...] = (act * up).astype(BF16)
    dgu_ref[:, :FT] = (dmix * up * sig * (1.0 + gate * (1.0 - sig))).astype(BF16)
    dgu_ref[:, FT:] = (dmix * act).astype(BF16)


def ffn_chunk(w, dy, w13, w2):
    rows, dim = w.shape
    cols = w2.shape[0]
    bm = 512
    return pl.pallas_call(
        ffn_kernel,
        grid=(cols // FT, rows // bm),
        in_specs=[
            pl.BlockSpec((bm, dim), lambda f, i: (i, 0)),
            pl.BlockSpec((bm, dim), lambda f, i: (i, 0)),
            pl.BlockSpec((dim, 2 * FT), lambda f, i: (0, f)),
            pl.BlockSpec((FT, dim), lambda f, i: (f, 0)),
        ],
        out_specs=[pl.BlockSpec((bm, FT), lambda f, i: (i, f)), pl.BlockSpec((bm, 2 * FT), lambda f, i: (i, f))],
        out_shape=[jax.ShapeDtypeStruct((rows, cols), BF16), jax.ShapeDtypeStruct((rows, 2 * cols), BF16)],
        compiler_params=pltpu.CompilerParams(vmem_limit_bytes=VMEM_LIMIT),
        cost_estimate=cost(6 * rows * dim * cols, 2 * (4 * rows * dim + 3 * dim * cols + 3 * rows * cols), rows * cols),
        name="ffn_chunk",
    )(w, dy, w13, w2)


def rms_backward(grad_normed, rows_f32, gain_f32):
    row_scale = lax.rsqrt(jnp.mean(rows_f32 * rows_f32, axis=-1, keepdims=True) + EPS)
    unit_rows = rows_f32 * row_scale
    gain_grad = jnp.sum(grad_normed * unit_rows, axis=0)
    grad_unit = grad_normed * gain_f32
    inner_mean = jnp.mean(grad_unit * unit_rows, axis=-1, keepdims=True)
    return row_scale * (grad_unit - unit_rows * inner_mean), gain_grad


def solution(mesh):
    flat_axes = ("dp", "sp")
    row_spec = P("dp", "sp", None)
    pos_spec = P("dp", "sp")
    vec_spec = P(flat_axes)
    mat_spec = P(flat_axes, None)
    cube_spec = P(flat_axes, None, None)
    n_dp = mesh.shape["dp"]

    def swap(values):
        return lax.ppermute(values, "sp", [(0, 1), (1, 0)])

    def gather_dp(values):
        return lax.all_gather(values, "dp", axis=0, tiled=True)

    def gather_all(values):
        return lax.all_gather(values, flat_axes, axis=0, tiled=True)

    def scatter_dp(values):
        return lax.psum_scatter(values, "dp", scatter_dimension=0, tiled=True)

    def scatter_all(values):
        return lax.psum_scatter(values, flat_axes, scatter_dimension=0, tiled=True)

    def layer(act_in, positions, out_grad, norm1_gain, norm2_gain, w_query, w_key, w_value, w_out, w_gate, w_up, w_down):
        core = lax.axis_index("sp")
        first = core == 0
        core_arr = jnp.full((1,), core, jnp.int32)
        rows = act_in.shape[1]
        shard = w_query.shape[0]
        n_head = w_query.shape[1]
        n_kv = w_key.shape[1]
        hpc = n_head // n_kv
        qw = hpc * HD
        fshard = w_down.shape[0]
        x = act_in[0]
        dy = out_grad[0]

        def in_order(mine, other, axis):
            return jnp.where(first, jnp.concatenate([mine, other], axis), jnp.concatenate([other, mine], axis))

        wq = w_query.reshape(shard, n_head * HD)
        parts = []
        for g in range(n_kv):
            parts += [wq[:, g * qw:(g + 1) * qw], w_key[:, g, :], w_value[:, g, :]]
        parts += [norm1_gain[:, None], norm2_gain[:, None], jnp.zeros((shard, HD - 2), BF16)]
        packed = gather_all(jnp.concatenate(parts, axis=1))
        n_qkv = n_kv * (qw + 2 * HD)
        w_qkv = packed[:, :n_qkv]
        gain1 = packed[:, n_qkv].astype(F32)
        gain2 = packed[:, n_qkv + 1].astype(F32)
        wo = gather_all(w_out)

        r_cuts = ((0, fshard * 3 // 7), (fshard * 3 // 7, fshard))

        def columns(mat, part, cut):
            return jnp.concatenate([mat[:, (2 * d + part) * fshard + cut[0]:(2 * d + part) * fshard + cut[1]] for d in range(n_dp)], axis=1)

        def pack13(part, cut):
            gate = columns(w_gate, part, cut)
            up = columns(w_up, part, cut)
            tiles = []
            for t in range(gate.shape[1] // FT):
                tiles += [gate[:, t * FT:(t + 1) * FT], up[:, t * FT:(t + 1) * FT]]
            return jnp.concatenate(tiles, axis=1)

        w13 = []
        w2 = []
        for cut in r_cuts:
            pack_a = pack13(0, cut)
            pack_b = pack13(1, cut)
            mine = jnp.where(first, pack_a, pack_b)
            other = jnp.where(first, pack_b, pack_a)
            w13.append(gather_dp(in_order(mine, swap(other), 0)))
            w2.append(gather_dp(w_down[cut[0]:cut[1]]))

        dy_full = jnp.concatenate([dy, swap(dy)], axis=0)
        pos_full = jnp.concatenate([positions[0], swap(positions[0])], axis=0)
        inv_freq = ROPE_BASE ** (-(jnp.arange(HD // 2, dtype=F32) * (2.0 / HD)))
        angles = pos_full.astype(F32)[:, None] * inv_freq[None, :]
        cos_h = jnp.cos(angles)
        sin_h = jnp.sin(angles)
        cos = jnp.concatenate([cos_h, cos_h], axis=1)
        sin = jnp.concatenate([-sin_h, sin_h], axis=1)

        qkv, normed_a = qkv_project(x, gain1[None, :], w_qkv, cos, sin)
        half = n_qkv // 2
        qkv_mine = jnp.where(first, qkv[:, :half], qkv[:, half:])
        qkv_other = jnp.where(first, qkv[:, half:], qkv[:, :half])
        qkv_seq = jnp.concatenate([qkv_mine, swap(qkv_other)], axis=0)
        attn_seq, lse = attn_forward(core_arr, qkv_seq)
        attn_flat = in_order(attn_seq[:rows], swap(attn_seq[rows:]), 1)
        x_f = x.astype(F32)
        hidden = (x_f + dot(attn_flat, wo)).astype(BF16)
        hidden_f = hidden.astype(F32)
        scale_b = lax.rsqrt(jnp.mean(hidden_f * hidden_f, axis=-1, keepdims=True) + EPS)
        normed_b = (hidden_f * scale_b * gain2).astype(BF16)
        normed_full = jnp.concatenate([normed_b, swap(normed_b)], axis=0)

        tn = (((0,), (0,)), ((), ()))
        mixed = []
        dgu = []
        down_parts = []
        gu_parts = []
        for k in range(len(r_cuts)):
            mix_k, dgu_k = ffn_chunk(normed_full, dy_full, w13[k], w2[k])
            mixed.append(mix_k)
            dgu.append(dgu_k)
            down_k = lax.dot_general(mix_k, dy_full, tn, preferred_element_type=F32)
            gu_k = lax.dot_general(normed_full, dgu_k, tn, preferred_element_type=F32)
            down_parts.append(scatter_dp(down_k))
            gu_parts.append(scatter_dp(gu_k))

        def grad_normed_part(lo, hi):
            return sum(dot_nt(dgu[k][lo:hi], w13[k]) for k in range(len(r_cuts)))

        grad_other = grad_normed_part(rows, 2 * rows)
        grad_other = swap(grad_other)
        grad_normed_b = (grad_normed_part(0, rows) + grad_other).astype(BF16).astype(F32)
        grad_rows_b, gain2_grad = rms_backward(grad_normed_b, hidden_f, gain2)
        grad_hidden = (dy.astype(F32) + grad_rows_b).astype(BF16)

        grad_attn = dot_nt(grad_hidden, wo).astype(BF16)
        ga_mine = jnp.where(first, grad_attn[:, :qw], grad_attn[:, qw:])
        ga_other = jnp.where(first, grad_attn[:, qw:], grad_attn[:, :qw])
        grad_attn_seq = jnp.concatenate([ga_mine, swap(ga_other)], axis=0)
        wout_part = lax.dot_general(attn_flat, grad_hidden, tn, preferred_element_type=F32)
        wout_grad = scatter_all(wout_part)
        dq, dkv = attn_backward(core_arr, qkv_seq, grad_attn_seq, attn_seq, lse, cos, sin)
        dqkv_mine = jnp.concatenate([dq[:rows], dkv[:rows]], axis=1)
        dqkv_other = swap(jnp.concatenate([dq[rows:], dkv[rows:]], axis=1))
        dqkv = in_order(dqkv_mine, dqkv_other, 1)
        qkv_part = lax.dot_general(normed_a, dqkv, tn, preferred_element_type=F32)
        qkv_grad = scatter_all(qkv_part)
        grad_normed_a = dot_nt(dqkv, w_qkv).astype(BF16).astype(F32)
        grad_rows_a, gain1_grad = rms_backward(grad_normed_a, x_f, gain1)
        in_grad = (grad_hidden.astype(F32) + grad_rows_a).astype(BF16)
        gain_grads = (scatter_all(gain1_grad), scatter_all(gain2_grad))

        def out_part(lo, hi):
            return sum(dot(mixed[k][lo:hi], w2[k]) for k in range(len(r_cuts)))

        out_other = out_part(rows, 2 * rows)
        act_out = (hidden_f + out_part(0, rows) + swap(out_other)).astype(BF16)

        down_grad = jnp.concatenate(down_parts, axis=0)
        gate_cols = []
        up_cols = []
        for k, cut in enumerate(r_cuts):
            top = gu_parts[k][:shard]
            bottom = gu_parts[k][shard:]
            mine = jnp.where(first, top, bottom)
            other = swap(jnp.where(first, bottom, top))
            by_core = (jnp.where(first, mine, other), jnp.where(first, other, mine))
            width = cut[1] - cut[0]
            gate_k = []
            up_k = []
            for arr in by_core:
                tiles = range(arr.shape[1] // (2 * FT))
                gate_k.append(jnp.concatenate([arr[:, 2 * t * FT:(2 * t + 1) * FT] for t in tiles], axis=1))
                up_k.append(jnp.concatenate([arr[:, (2 * t + 1) * FT:(2 * t + 2) * FT] for t in tiles], axis=1))
            gate_cols.append((gate_k, width))
            up_cols.append((up_k, width))

        def interleave(cols):
            pieces = []
            for d in range(n_dp):
                for part in range(2):
                    for arrs, width in cols:
                        pieces.append(arrs[part][:, d * width:(d + 1) * width])
            return jnp.concatenate(pieces, axis=1)

        gate_grad = interleave(gate_cols)
        up_grad = interleave(up_cols)
        per = qw + 2 * HD
        query_grad = jnp.concatenate([qkv_grad[:, g * per:g * per + qw] for g in range(n_kv)], axis=1).reshape(shard, n_head, HD)
        key_grad = jnp.stack([qkv_grad[:, g * per + qw:g * per + qw + HD] for g in range(n_kv)], axis=1)
        value_grad = jnp.stack([qkv_grad[:, g * per + qw + HD:(g + 1) * per] for g in range(n_kv)], axis=1)
        return (act_out[None], in_grad[None], gain_grads[0], gain_grads[1], query_grad, key_grad, value_grad, wout_grad, gate_grad, up_grad, down_grad)

    return jax.shard_map(layer, mesh=mesh, in_specs=(row_spec, pos_spec, row_spec, vec_spec, vec_spec, cube_spec, cube_spec, cube_spec, mat_spec, mat_spec, mat_spec, mat_spec), out_specs=(row_spec, row_spec, vec_spec, vec_spec, cube_spec, cube_spec, cube_spec, mat_spec, mat_spec, mat_spec, mat_spec), check_vma=False)
```

time: 3740 us -> 1450 us (0.39)
  matrix products: 2040 us -> 556 us
  waiting for transfers between devices: 701 us -> 54.3 us
  Pallas kernels: 0 us -> 603 us
  other arithmetic: 599 us -> 120 us
  local copies, waits for them, and re-layouts: 219 us -> 67.4 us
  blocking collectives: 139 us -> 22.8 us
    dot_general x133 -> x17, matrix products: 2040 us -> 556 us  [the longest x6 192 us: dot_nt(): return lax.dot_general(a, b, NT, preferred_element_type=F32)]
    reduce_scatter x7 -> x6, waiting for transfers between devices: 698 us -> 0.02 us  [the longest x2 0.01 us: scatter_all(): return lax.psum_scatter(values, flat_axes, scatter_dimension=0, tiled=True)]
    pallas_call x0 -> x5, Pallas kernels: none -> 603 us  [the longest x2 219 us: ffn_chunk(): pl.pallas_call(ffn_kernel, grid=(cols // FT, rows // bm), in_specs=[pl.Bl...]
    another operation x19 -> x2, other arithmetic: 290 us -> 0.03 us  [the longest x1 0.02 us: layer(): jnp.stack([qkv_grad[:, g * per + qw:g * per + qw + HD] for g in range(n_k...]
    reduce_sum x17 -> x1, other arithmetic: 199 us -> 4.23 us  [rms_backward(): jnp.mean(rows_f32 * rows_f32, axis=-1, keepdims=True) + EPS]
    while x34 -> x0, local copies, waits for them, and re-layouts: 87.2 us -> none
    all_to_all x6 -> x0, blocking collectives: 58.1 us -> none  [the longest x4 33.6 us: to_tokens(): return lax.all_to_all(values, 'sp', 1, 2, tiled=True)]
    unnamed x104 -> x74, local copies, waits for them, and re-layouts: 57.1 us -> 9.05 us
  transfers between devices with their start and end apart: 14 -> 25, of which waited for: 3 -> 8; matrix products, arithmetic and copies ran while one was open for 34% -> 51% of each run, Pallas kernels for 0% -> 42%
where the time goes in v1:
time: 1450 us; the launch traced here: 1440 us
  Pallas kernels  603 us (42%)
  matrix products  556 us (38%)
  other arithmetic  120 us (8%)
  local copies, waits for them, and re-layouts  67.4 us (5%)
  waiting for transfers between devices  54.3 us (4%)
  blocking collectives  22.8 us (2%)
  between operations  15.2 us (1%)
    pallas_call x2, Pallas kernels, ffn_chunk(): pl.pallas_call(ffn_kernel, grid=(cols // FT, rows // bm), in_specs=[pl.Bl...  219 us
    pallas_call x1, Pallas kernels, attn_forward(): pl.pallas_call(attn_fwd_kernel, grid_spec=pltpu.PrefetchScalarGridSpec(nu...  196 us
    dot_general x6, matrix products, dot_nt(): return lax.dot_general(a, b, NT, preferred_element_type=F32)  192 us
    pallas_call x1, Pallas kernels, attn_backward(): pl.pallas_call(attn_bwd_kernel, grid_spec=pltpu.PrefetchScalarGridSpec(nu...  167 us
    dot_general x2, matrix products, layer(): gu_k = lax.dot_general(normed_full, dgu_k, tn, preferred_element_type=F32)  138 us
    dot_general x5, matrix products, dot(): return jnp.dot(a, b, preferred_element_type=F32)  110 us
    dot_general x2, matrix products, layer(): down_k = lax.dot_general(mix_k, dy_full, tn, preferred_element_type=F32)  76.8 us
    ppermute x13, waiting for transfers between devices, swap(): return lax.ppermute(values, 'sp', [(0, 1), (1, 0)])  37 us
  transfers between devices with their start and end apart: 25, of which 8 were waited for; matrix products, arithmetic and copies ran while one was open for 51% of the time, Pallas kernels for 42%

profile of v1, /device:TPU:0, one launch (start us, length us, event | category | flops | bytes accessed | tf_op | source)
XLA Modules:
  0.0 1444.5 jit_solution(5943828832300591121)
XLA Ops:
  30.7 7.5 fusion.49
  38.2 3.2 pad_maximum_fusion.6
  41.4 16.4 %all-gather.7.cloned.1.call-done = bf16[1536,2176]{1,0:T(8,128)(2,1)} async-done(((bf16[192,2176]{1,0:T(8,128)(2,1)}), bf16[1536,2176]{1,0:T(8,128)(2,1)}) %all-gather.7.cloned.1.call-update) | async-done | bytes 6684688 | tf_op jit(solution)/shard_map/all_gather | solution.py:350
  60.0 6.6 slice.543.w_ref
  66.6 20.6 %qkv_project.1 = (bf16[2048,2048]{1,0:T(8,128)(2,1)}, bf16[2048,1536]{1,0:T(8,128)(2,1)}) custom-call(bf16[2048,1536]{1,0:T(8,128)(2,1)} %bitcast.61, f32[1,1536]{1,0:T(1,128)} %reshape.98.g_ref, bf16[1536,2048]{1,0:T(8,128)(2,1)} %slice.543.w_ref, f32[4096,128]{1,0:T(8,128)} %get-tuple-element.181.cos_ref.cos_all_ref, ...), custom_call_target="tpu_custom_call" | custom-call | flops 12884901888 | bytes 27262976 | tf_op jit(solution)/shard_map/qkv_project/pallas_call | solution.py:57
  87.2 6.4 broadcast_select_fusion.1
  95.4 5.7 collective-permute-done.1
  101.2 8.0 pad_maximum_fusion.2.q_ref.k_ref.v_ref
  109.2 196.2 %attn_forward.1 = (bf16[4096,768]{1,0:T(8,128)(2,1)}, f32[16,8,256]{2,1,0:T(8,128)}) custom-call(s32[1]{0:T(128)} %bitcast.1.c_ref, bf16[4096,1024]{1,0:T(8,128)(2,1)} %pad_maximum_fusion.2.q_ref.k_ref.v_ref, bf16[4096,1024]{1,0:T(8,128)(2,1)} %pad_maximum_fusion.2.q_ref.k_ref.v_ref, bf16[4096,1024]{1,0:T(8,128)(2,1)} %pad_maximum_fusion.2.q_ref.k_ref.v_ref), custom_call_target="tpu_custom_call" | custom-call | flops 51539607552 | bytes 16777216 | tf_op jit(solution)/shard_map/attn_forward/pallas_call | solution.py:143
  305.4 6.1 fusion.71
  317.5 15.8 %fusion.30 = (f32[2048]{0:T(1024)S(1)}, bf16[2048,1536]{1,0:T(8,128)(2,1)S(1)}) fusion(bf16[1536,1536]{1,0:T(8,128)(2,1)} %all-gather.9.cloned.1.call-done, bf16[2048,768]{1,0:T(8,128)(2,1)} %collective-permute-done.2, bf16[2048,768]{1,0:T(8,128)(2,1)} %get-tuple-element.82, pred[]{:T(512)S(6)} %eq.3, bf16[1,2048,1536]{2,1,0:T(8,128)(2,1)} %param.12), kind=kOutput, calls=%fused_computation.38 | convolution fusion | flops 9710860288 | bytes 23601152 | tf_op jit(solution)/shard_map/dot_general | solution.py:22
  333.3 4.2 fusion.27
  338.8 12.4 collective-permute-done.6
  353.9 11.2 pad_maximum_fusion.1.dy_ref
  365.1 11.1 pad_maximum_fusion.w_ref
  376.1 94.3 %ffn_chunk.2 = (bf16[4096,1920]{1,0:T(8,128)(2,1)}, bf16[4096,3840]{1,0:T(8,128)(2,1)}) custom-call(bf16[4096,1536]{1,0:T(8,128)(2,1)} %pad_maximum_fusion.w_ref, bf16[4096,1536]{1,0:T(8,128)(2,1)} %pad_maximum_fusion.1.dy_ref, bf16[1536,3840]{1,0:T(8,128)(2,1)} %all-gather.11.cloned.1.call-done.w13_ref, bf16[1920,1536]{1,0:T(8,128)(2,1)} %all-gather.13.cloned.1.call-done.w2_ref), custom_call_target="tpu_custom_call" | custom-call | flops 72477573120 | bytes 115212288 | tf_op jit(solution)/shard_map/ffn_chunk/pallas_call | solution.py:308
  470.4 60.9 %fusion.69 = f32[1536,3840]{1,0:T(8,128)} fusion(bf16[4096,3840]{1,0:T(8,128)(2,1)} %get-tuple-element.25, bf16[2048,1536]{1,0:T(8,128)(2,1)} %collective-permute-done.3, bf16[2048,1536]{1,0:T(8,128)(2,1)} %fusion.27), kind=kOutput, calls=%fused_computation.162 | convolution fusion | flops 48343547904 | bytes 67633152 | tf_op jit(solution)/shard_map/dot_general | solution.py:443
  531.4 125.2 %ffn_chunk.3 = (bf16[4096,2560]{1,0:T(8,128)(2,1)}, bf16[4096,5120]{1,0:T(8,128)(2,1)}) custom-call(bf16[4096,1536]{1,0:T(8,128)(2,1)} %pad_maximum_fusion.w_ref, bf16[4096,1536]{1,0:T(8,128)(2,1)} %pad_maximum_fusion.1.dy_ref, bf16[1536,5120]{1,0:T(8,128)(2,1)} %all-gather.15.cloned.1.call-done.w13_ref, bf16[2560,1536]{1,0:T(8,128)(2,1)} %all-gather.17.cloned.1.call-done.w2_ref), custom_call_target="tpu_custom_call" | custom-call | flops 96636764160 | bytes 136839168 | tf_op jit(solution)/shard_map/ffn_chunk/pallas_call | solution.py:308
  656.6 76.7 %fusion.68 = f32[1536,5120]{1,0:T(8,128)} fusion(bf16[4096,5120]{1,0:T(8,128)(2,1)} %get-tuple-element.26, bf16[2048,1536]{1,0:T(8,128)(2,1)} %collective-permute-done.3, bf16[2048,1536]{1,0:T(8,128)(2,1)} %fusion.27), kind=kOutput, calls=%fused_computation.161 | convolution fusion | flops 64449675264 | bytes 85983232 | tf_op jit(solution)/shard_map/dot_general | solution.py:443
  733.4 34.1 %fusion.67 = f32[1920,1536]{1,0:T(8,128)} fusion(bf16[4096,1920]{1,0:T(8,128)(2,1)} %get-tuple-element.23, bf16[2048,1536]{1,0:T(8,128)(2,1)} %collective-permute-done.4, bf16[2048,1536]{1,0:T(8,128)(2,1)} %bitcast.64), kind=kOutput, calls=%fused_computation.160 | convolution fusion | flops 24184356864 | bytes 40108032 | tf_op jit(solution)/shard_map/dot_general | solution.py:442
  767.6 42.6 %fusion = f32[2048,1536]{1,0:T(8,128)} fusion(bf16[1536,5120]{1,0:T(8,128)(2,1)} %all-gather.15.cloned.1.call-done.w13_ref, bf16[4096,5120]{1,0:T(8,128)(2,1)} %get-tuple-element.26), kind=kOutput, calls=%fused_computation | convolution fusion | flops 32212254720 | bytes 49283072 | tf_op jit(solution)/shard_map/dot_general | solution.py:26
  810.2 33.7 %fusion.39 = f32[2048,1536]{1,0:T(8,128)} fusion(f32[2048,1536]{1,0:T(8,128)} %fusion, bf16[1536,3840]{1,0:T(8,128)(2,1)} %all-gather.11.cloned.1.call-done.w13_ref, bf16[4096,3840]{1,0:T(8,128)(2,1)} %get-tuple-element.25), kind=kOutput, calls=%fused_computation.48 | convolution fusion | flops 24162336768 | bytes 52690944 | tf_op jit(solution)/shard_map/dot_general | solution.py:26
  844.1 42.7 %fusion.66 = f32[2560,1536]{1,0:T(8,128)} fusion(bf16[4096,2560]{1,0:T(8,128)(2,1)} %get-tuple-element.24, bf16[2048,1536]{1,0:T(8,128)(2,1)} %collective-permute-done.4, bf16[2048,1536]{1,0:T(8,128)(2,1)} %bitcast.65), kind=kOutput, calls=%fused_computation.159 | convolution fusion | flops 32237420544 | bytes 49283072 | tf_op jit(solution)/shard_map/dot_general | solution.py:442
  886.9 42.8 %fusion.2 = f32[2048,1536]{1,0:T(8,128)} fusion(bf16[1536,5120]{1,0:T(8,128)(2,1)} %all-gather.15.cloned.1.call-done.w13_ref, bf16[4096,5120]{1,0:T(8,128)(2,1)} %get-tuple-element.26), kind=kOutput, calls=%fused_computation.2 | convolution fusion | flops 32212254720 | bytes 49283072 | tf_op jit(solution)/shard_map/dot_general | solution.py:26
  929.7 40.2 %fusion.29 = (f32[1536]{0:T(1024)}, f32[2048]{0:T(1024)S(1)}, bf16[2048,1536]{1,0:T(8,128)(2,1)}) fusion(bf16[2048,1536]{1,0:T(8,128)(2,1)} %copy-done.2, f32[2048]{0:T(1024)S(1)} %copy-done.21, f32[1536]{0:T(1024)S(1)} %copy-done.17, f32[2048,1536]{1,0:T(8,128)} %collective-permute-done.8, f32[2048,1536]{1,0:T(8,128)} %fusion.2, ...), kind=kOutput, calls=%fused_computation.37 | convolution fusion | flops 24193789952 | bytes 65302528 | tf_op jit(solution)/shard_map/dot_general | solution.py:26
  969.9 8.8 fusion.22
  978.7 11.3 convolution_convert_fusion.1
  991.8 5.3 collective-permute-done.9
  1000.2 167.1 %attn_backward.1 = (bf16[4096,768]{1,0:T(8,128)(2,1)}, bf16[4096,256]{1,0:T(8,128)(2,1)}) custom-call(s32[1]{0:T(128)} %bitcast.1.c_ref, bf16[4096,1024]{1,0:T(8,128)(2,1)} %pad_maximum_fusion.2.q_ref.k_ref.v_ref, bf16[4096,768]{1,0:T(8,128)(2,1)} %pad_maximum_fusion.4.do_ref, bf16[4096,768]{1,0:T(8,128)(2,1)} %get-tuple-element.22.o_ref, ...), custom_call_target="tpu_custom_call" | custom-call | flops 128849018880 | bytes 33554432 | tf_op jit(solution)/shard_map/attn_backward/pallas_call | solution.py:256
  1168.9 4.0 fusion.70
  1173.6 7.1 collective-permute-done.10
  1182.8 22.8 %fusion.65 = f32[1536,2048]{1,0:T(8,128)} fusion(bf16[2048,1536]{1,0:T(8,128)(2,1)} %get-tuple-element.30, bf16[2048,1024]{1,0:T(8,128)(2,1)} %copy-done.25, bf16[2048,256]{1,0:T(8,128)(2,1)S(1)} %get-tuple-element.148, bf16[2048,768]{1,0:T(8,128)(2,1)S(1)} %get-tuple-element.78, pred[]{:T(512)S(6)} %eq.3), kind=kOutput, calls=%fused_computation.158 | convolution fusion | flops 12939427840 | bytes 27262976 | tf_op jit(solution)/shard_map/dot_general | solution.py:466
  1205.6 23.3 %fusion.33 = f32[2048,1536]{1,0:T(8,128)} fusion(bf16[2560,1536]{1,0:T(8,128)(2,1)} %all-gather.17.cloned.1.call-done.w2_ref, bf16[4096,2560]{1,0:T(8,128)(2,1)} %get-tuple-element.24), kind=kOutput, calls=%fused_computation.44 | convolution fusion | flops 16106127360 | bytes 30932992 | tf_op jit(solution)/shard_map/dot_general | solution.py:22
  1228.9 22.1 %convolution_add_fusion = f32[2048,1536]{1,0:T(8,128)} fusion(f32[2048,1536]{1,0:T(8,128)} %fusion.33, bf16[1920,1536]{1,0:T(8,128)(2,1)} %all-gather.13.cloned.1.call-done.w2_ref, bf16[4096,1920]{1,0:T(8,128)(2,1)} %get-tuple-element.23), kind=kOutput, calls=%fused_computation.49 | convolution fusion | flops 12082741248 | bytes 38928384 | tf_op jit(solution)/shard_map/dot_general | solution.py:22
  1251.0 4.2 fusion.26
  1255.3 23.1 %fusion.35 = f32[2048,1536]{1,0:T(8,128)} fusion(bf16[2560,1536]{1,0:T(8,128)(2,1)} %all-gather.17.cloned.1.call-done.w2_ref, bf16[4096,2560]{1,0:T(8,128)(2,1)} %get-tuple-element.24), kind=kOutput, calls=%fused_computation.46 | convolution fusion | flops 16106127360 | bytes 30932992 | tf_op jit(solution)/shard_map/dot_general | solution.py:22
  1278.4 17.8 %fusion.48 = f32[1536,1536]{1,0:T(8,128)} fusion(bf16[2048,1536]{1,0:T(8,128)(2,1)S(1)} %bitcast.67, bf16[2048,768]{1,0:T(8,128)(2,1)} %collective-permute-done.2, bf16[2048,768]{1,0:T(8,128)(2,1)S(1)} %copy-done.7, pred[]{:T(512)S(6)} %eq.3), kind=kOutput, calls=%fused_computation.86 | convolution fusion | flops 9691987968 | bytes 22020096 | tf_op jit(solution)/shard_map/dot_general | solution.py:460
  1296.3 25.4 %fusion.44 = bf16[1,2048,1536]{2,1,0:T(8,128)(2,1)} fusion(f32[2048,1536]{1,0:T(8,128)} %collective-permute-done.7, f32[2048,1536]{1,0:T(8,128)} %fusion.35, bf16[1920,1536]{1,0:T(8,128)(2,1)} %all-gather.13.cloned.1.call-done.w2_ref, bf16[4096,1920]{1,0:T(8,128)(2,1)} %get-tuple-element.23, bf16[2048,1536]{1,0:T(8,128)(2,1)} %copy-done.2), kind=kOutput, calls=%fused_computation.57 | convolution fusion | flops 12095324160 | bytes 51511296 | tf_op jit(solution)/shard_map/dot_general | solution.py:22
  1321.7 21.3 %fusion.24 = (f32[1536]{0:T(1024)S(1)}, f32[2048]{0:T(1024)S(1)}, bf16[2048,1536]{1,0:T(8,128)(2,1)}) fusion(f32[2048]{0:T(1024)S(1)} %add_rsqrt_fusion, bf16[1,2048,1536]{2,1,0:T(8,128)(2,1)} %param.12, f32[1536]{0:T(1024)S(1)} %copy-done.19, bf16[1536,2176]{1,0:T(8,128)(2,1)} %all-gather.7.cloned.1.call-done, bf16[2048,1024]{1,0:T(8,128)(2,1)} %copy-done.25, ...), kind=kOutput, calls=%fused_computation.32 | convolution fusion | flops 12967735296 | bytes 27291648 | tf_op jit(solution)/shard_map/dot_general | solution.py:26
  1343.0 22.8 %all-reduce.2 = (f32[1536]{0:T(1024)S(1)}, f32[1536]{0:T(1024)S(1)}) all-reduce(f32[1536]{0:T(1024)S(1)} %get-tuple-element.66, f32[1536]{0:T(1024)S(1)} %copy-done.22), channel_id=2, replica_groups=mesh['dp'=4,'sp'=2] {'dp','sp'}, use_global_device_ids=true, to_apply=%region_5.6.clone | all-reduce | flops 3072 | bytes 24576
  1367.1 12.0 fusion.47
  1379.1 4.9 slice_select_fusion.2
  1384.0 5.9 slice_select_fusion
  1390.6 6.5 pad_maximum_fusion.3
  1402.3 3.5 broadcast_select_fusion.8
  1414.0 3.3 broadcast_select_fusion.4
  1420.4 8.8 concatenate.191
  1429.2 8.1 concatenate.196
  (191 shorter events, 65.4 us)
Async XLA Ops:
  7.2 50.6 %all-gather.7.cloned.1.call-start = ((), (), s32[]{:S(2)}) async-start(), calls=%async_computation.6 | async-start | bytes 7520256 | tf_op jit(solution)/shard_map/all_gather | solution.py:350
  13.3 301.4 %all-gather.9.cloned.1.call-start = ((), (), s32[]{:S(2)}) async-start(), calls=%async_computation.7 | async-start | bytes 5308416 | tf_op jit(solution)/shard_map/all_gather | solution.py:350
  14.1 362.1 %all-gather.13.cloned.1.call-start = ((), (), s32[]{:S(2)}) async-start(), calls=%async_computation.9 | async-start | bytes 7372800 | tf_op jit(solution)/shard_map/all_gather | solution.py:347
  16.8 359.4 %all-gather.11.cloned.1.call-start = ((), (), s32[]{:S(2)}) async-start(), calls=%async_computation.8 | async-start | bytes 14745600 | tf_op jit(solution)/shard_map/all_gather | solution.py:347
  23.0 6.5 copy-start.23
  23.2 3.8 collective-permute-start.5
  29.0 502.3 %all-gather.17.cloned.1.call-start = ((), (), s32[]{:S(2)}) async-start(), calls=%async_computation.11 | async-start | bytes 9830400 | tf_op jit(solution)/shard_map/all_gather | solution.py:347
  29.5 1.2 collective-permute-start
  59.4 7.2 copy-start.18
  59.4 273.9 %copy-start.16 = (f32[1536]{0:T(1024)}, f32[1536]{0:T(1024)S(1)}, u32[]{:S(2)}) copy-start(f32[1536]{0:T(1024)S(1)} %get-tuple-element.68) | copy-start | bytes 18436
  87.2 6.7 copy-start.6
  93.7 7.5 collective-permute-start.1
  95.4 436.0 %all-gather.15.cloned.1.call-start = ((), (), s32[]{:S(2)}) async-start(), calls=%async_computation.10 | async-start | bytes 19660800 | tf_op jit(solution)/shard_map/all_gather | solution.py:347
  305.4 6.6 copy-start.4
  305.4 6.8 copy-start.5
  311.5 6.0 collective-permute-start.2
  311.8 42.1 %collective-permute-start.4 = (bf16[2048,1536]{1,0:T(8,128)(2,1)}, bf16[2048,1536]{1,0:T(8,128)(2,1)}, u32[]{:S(2)}, u32[]{:S(2)}) collective-permute-start(bf16[2048,1536]{1,0:T(8,128)(2,1)} %bitcast.62), channel_id=1, source_target_pairs={{0,1},{1,0},{2,3},{3,2},{4,5},{5,4},{6,7},{7,6}} | collective-permute-start | bytes 18874376 | tf_op jit(solution)/shard_map/ppermute | solution.py:344
  338.0 27.1 %collective-permute-start.3 = (bf16[2048,1536]{1,0:T(8,128)(2,1)}, bf16[2048,1536]{1,0:T(8,128)(2,1)}, u32[]{:S(2)}, u32[]{:S(2)}) collective-permute-start(bf16[2048,1536]{1,0:T(8,128)(2,1)} %fusion.27), channel_id=1, source_target_pairs={{0,1},{1,0},{2,3},{3,2},{4,5},{5,4},{6,7},{7,6}} | collective-permute-start | bytes 18874376 | tf_op jit(solution)/shard_map/ppermute | solution.py:344
  338.5 12.6 collective-permute-start.6
  353.8 1025.3 %reduce-scatter.11.cloned.1.call-start = ((), (), s32[]{:S(2)}) async-start(), calls=%async_computation.14 | async-start | bytes 29491200 | tf_op jit(solution)/shard_map/reduce_scatter | solution.py:353
  531.3 852.7 %reduce-scatter.13.cloned.1.call-start = ((), (), s32[]{:S(2)}) async-start(), calls=%async_computation.15 | async-start | bytes 39321600 | tf_op jit(solution)/shard_map/reduce_scatter | solution.py:353
  733.3 657.2 %reduce-scatter.15.cloned.1.call-start = ((), (), s32[]{:S(2)}) async-start(), calls=%async_computation.16 | async-start | bytes 14745600 | tf_op jit(solution)/shard_map/reduce_scatter | solution.py:353
  767.5 623.1 %reduce-scatter.17.cloned.1.call-start = ((), (), s32[]{:S(2)}) async-start(), calls=%async_computation.17 | async-start | bytes 19660800 | tf_op jit(solution)/shard_map/reduce_scatter | solution.py:353
  843.9 85.8 %collective-permute-start.8 = (f32[2048,1536]{1,0:T(8,128)}, f32[2048,1536]{1,0:T(8,128)}, u32[]{:S(2)}, u32[]{:S(2)}) collective-permute-start(f32[2048,1536]{1,0:T(8,128)} %fusion.39), channel_id=1, source_target_pairs={{0,1},{1,0},{2,3},{3,2},{4,5},{5,4},{6,7},{7,6}} | collective-permute-start | bytes 37748744 | tf_op jit(solution)/shard_map/ppermute | solution.py:344
  886.8 42.9 %copy-start.17 = (f32[1536]{0:T(1024)S(1)}, f32[1536]{0:T(1024)}, u32[]{:S(2)}) copy-start(f32[1536]{0:T(1024)} %copy-done.16) | copy-start | bytes 18436
  886.8 42.9 %copy-start.21 = (f32[2048]{0:T(1024)S(1)}, f32[2048]{0:T(1024)}, u32[]{:S(2)}) copy-start(f32[2048]{0:T(1024)} %copy-done.20) | copy-start | bytes 24580
  886.8 510.3 %reduce-scatter.7.cloned.1.call-start = ((), (), s32[]{:S(2)}) async-start(), calls=%async_computation.12 | async-start | bytes 14155776 | tf_op jit(solution)/shard_map/reduce_scatter | solution.py:356
  969.9 8.8 copy-start.24
  978.7 11.3 copy-start.3
  990.6 6.5 collective-permute-start.9
  1168.9 13.8 copy-start.14
  1173.0 9.8 copy-start.8
  1173.6 7.2 collective-permute-start.10
  1205.6 231.8 %reduce-scatter.9.cloned.1.call-start = ((), (), s32[]{:S(2)}) async-start(), calls=%async_computation.13 | async-start | bytes 10616832 | tf_op jit(solution)/shard_map/reduce_scatter | solution.py:356
  1250.9 45.3 %collective-permute-start.7 = (f32[2048,1536]{1,0:T(8,128)}, f32[2048,1536]{1,0:T(8,128)}, u32[]{:S(2)}, u32[]{:S(2)}) collective-permute-start(f32[2048,1536]{1,0:T(8,128)} %convolution_add_fusion), channel_id=1, source_target_pairs={{0,1},{1,0},{2,3},{3,2},{4,5},{5,4},{6,7},{7,6}} | collective-permute-start | bytes 37748744 | tf_op jit(solution)/shard_map/ppermute | solution.py:344
  1251.0 27.4 %slice-start.2 = ((s8[6291456]{0:T(1024)(128)(4,1)}), s8[4194304]{0:T(1024)(128)(4,1)S(1)}, s32[]{:S(2)}) async-start(s8[6291456]{0:T(1024)(128)(4,1)} %bitcast.66), calls=%async_computation.20 | async-start | bytes 8388608
  1255.2 23.1 %slice-start.3 = ((s8[6291456]{0:T(1024)(128)(4,1)}), s8[2097152]{0:T(1024)(128)(4,1)S(1)}, s32[]{:S(2)}) async-start(s8[6291456]{0:T(1024)(128)(4,1)} %bitcast.66), calls=%async_computation.21 | async-start | bytes 4194304
  1255.2 23.1 %copy-start.7 = (bf16[2048,768]{1,0:T(8,128)(2,1)S(1)}, bf16[2048,768]{1,0:T(8,128)(2,1)}, u32[]{:S(2)}) copy-start(bf16[2048,768]{1,0:T(8,128)(2,1)} %get-tuple-element.82) | copy-start | bytes 9437188
  1296.2 25.5 %copy-start.9 = (bf16[2048,768]{1,0:T(8,128)(2,1)S(1)}, bf16[2048,768]{1,0:T(8,128)(2,1)}, u32[]{:S(2)}) copy-start(bf16[2048,768]{1,0:T(8,128)(2,1)} %copy-done.8) | copy-start | bytes 9437188
  1296.2 25.4 %copy-start.15 = (bf16[2048,256]{1,0:T(8,128)(2,1)S(1)}, bf16[2048,256]{1,0:T(8,128)(2,1)}, u32[]{:S(2)}) copy-start(bf16[2048,256]{1,0:T(8,128)(2,1)} %copy-done.14) | copy-start | bytes 3145732
  1296.2 25.4 %copy-start.19 = (f32[1536]{0:T(1024)S(1)}, f32[1536]{0:T(1024)}, u32[]{:S(2)}) copy-start(f32[1536]{0:T(1024)} %copy-done.18) | copy-start | bytes 18436
  1321.7 21.3 %copy-start.22 = (f32[1536]{0:T(1024)S(1)}, f32[1536]{0:T(1024)}, u32[]{:S(2)}) copy-start(f32[1536]{0:T(1024)} %get-tuple-element.64) | copy-start | bytes 18436
  1384.0 18.3 %collective-permute-start.11 = (f32[192,3840]{1,0:T(8,128)}, f32[192,3840]{1,0:T(8,128)S(1)}, u32[]{:S(2)}, u32[]{:S(2)}) collective-permute-start(f32[192,3840]{1,0:T(8,128)} %slice_select_fusion.2), channel_id=1, source_target_pairs={{0,1},{1,0},{2,3},{3,2},{4,5},{5,4},{6,7},{7,6}} | collective-permute-start | bytes 8847368 | tf_op jit(solution)/shard_map/ppermute | solution.py:344
  1389.9 24.0 %collective-permute-start.12 = (f32[192,5120]{1,0:T(8,128)}, f32[192,5120]{1,0:T(8,128)}, u32[]{:S(2)}, u32[]{:S(2)}) collective-permute-start(f32[192,5120]{1,0:T(8,128)} %slice_select_fusion), channel_id=1, source_target_pairs={{0,1},{1,0},{2,3},{3,2},{4,5},{5,4},{6,7},{7,6}} | collective-permute-start | bytes 11796488 | tf_op jit(solution)/shard_map/ppermute | solution.py:344
  1407.2 6.7 slice-start
  1420.4 8.8 copy-start.12
  1420.4 8.8 copy-start.13
  1429.2 8.2 copy-start.1
  (7 other events, 24.0 us)
Sparse Core Ops, SparseCore 0:
  13.4 44.2 all-gather.6
  59.6 33.2 all-gather.8
  94.6 61.1 all-gather.12
  157.5 110.2 all-gather.10
  269.4 77.6 all-gather.16
  353.9 143.3 all-gather.14
  531.4 203.7 reduce-scatter.10
  738.3 267.1 reduce-scatter.12
  1008.5 108.5 reduce-scatter.14
  1120.1 140.7 reduce-scatter.16
  1264.3 84.4 reduce-scatter.6
  1352.6 68.4 reduce-scatter.8

commit v2 on v1

--- a/solution.py
+++ b/solution.py
@@ -73,6 +73,7 @@
 
 
 BQ = 256
+BQF = 512
 BK = 512
 
 
@@ -100,8 +101,8 @@
         k_blk = k_ref[pl.ds(phys(j), BK), :]
         vt = vt_ref[j]
         if masked:
-            keys = j * BK + lax.broadcasted_iota(jnp.int32, (BK, BQ), 0)
-            queries = i * BQ + lax.broadcasted_iota(jnp.int32, (BK, BQ), 1)
+            keys = j * BK + lax.broadcasted_iota(jnp.int32, (BK, BQF), 0)
+            queries = i * BQF + lax.broadcasted_iota(jnp.int32, (BK, BQF), 1)
             allowed = keys <= queries
         for h in range(n_head):
             t = dot_nt(k_blk, q_ref[:, h * HD:(h + 1) * HD]) * coef
@@ -115,7 +116,7 @@
             l_ref[h] = l_ref[h] * alpha + jnp.sum(p, axis=0, keepdims=True)
             acc_ref[h] = acc_ref[h] * alpha + dot(vt, p.astype(BF16))
 
-    last = (i * BQ) // BK
+    last = (i * BQF) // BK
 
     def body(j, carry):
         block(j, False)
@@ -134,7 +135,7 @@
     seq, width = qkv.shape
     qw = width - 2 * HD
     n_head = qw // HD
-    n_q = seq // BQ
+    n_q = seq // BQF
 
     def rows(i, c):
         return (lax.rem(i + c[0] * (n_q // 2), n_q), 0)
@@ -146,19 +147,19 @@
             num_scalar_prefetch=1,
             grid=(n_q,),
             in_specs=[
-                pl.BlockSpec((BQ, qw), rows),
+                pl.BlockSpec((BQF, qw), rows),
                 pl.BlockSpec((seq, HD), lambda i, c: (0, n_head)),
                 pl.BlockSpec((seq, HD), lambda i, c: (0, n_head + 1)),
             ],
-            out_specs=[pl.BlockSpec((BQ, qw), rows), pl.BlockSpec((1, 8, BQ), lambda i, c: (i, 0, 0))],
+            out_specs=[pl.BlockSpec((BQF, qw), rows), pl.BlockSpec((1, 8, BQF), lambda i, c: (i, 0, 0))],
             scratch_shapes=[
                 pltpu.VMEM((seq // BK, HD, BK), BF16),
-                pltpu.VMEM((n_head, 1, BQ), F32),
-                pltpu.VMEM((n_head, 1, BQ), F32),
-                pltpu.VMEM((n_head, HD, BQ), F32),
+                pltpu.VMEM((n_head, 1, BQF), F32),
+                pltpu.VMEM((n_head, 1, BQF), F32),
+                pltpu.VMEM((n_head, HD, BQF), F32),
             ],
         ),
-        out_shape=[jax.ShapeDtypeStruct((seq, qw), BF16), jax.ShapeDtypeStruct((n_q, 8, BQ), F32)],
+        out_shape=[jax.ShapeDtypeStruct((seq, qw), BF16), jax.ShapeDtypeStruct((n_q, 8, BQF), F32)],
         compiler_params=pltpu.CompilerParams(vmem_limit_bytes=VMEM_LIMIT),
         cost_estimate=cost(8 * pairs * HD, 4 * seq * width, pairs),
         name="attn_forward",
@@ -262,7 +263,7 @@
                 pl.BlockSpec((BQ, qw), rows),
                 pl.BlockSpec((BQ, qw), rows),
                 pl.BlockSpec((BQ, qw), rows),
-                pl.BlockSpec((1, 8, BQ), lambda i, c: (i, 0, 0)),
+                pl.BlockSpec((1, 8, BQ), lambda i, c: (i // (BQF // BQ), 0, lax.rem(i, BQF // BQ))),
                 pl.BlockSpec((BQ, HD), rows),
                 pl.BlockSpec((BQ, HD), rows),
                 pl.BlockSpec((seq, HD), lambda i, c: (0, n_head)),
@@ -339,6 +340,7 @@
     mat_spec = P(flat_axes, None)
     cube_spec = P(flat_axes, None, None)
     n_dp = mesh.shape["dp"]
+    n_all = n_dp * mesh.shape["sp"]
 
     def swap(values):
         return lax.ppermute(values, "sp", [(0, 1), (1, 0)])
@@ -460,15 +462,24 @@
         wout_part = lax.dot_general(attn_flat, grad_hidden, tn, preferred_element_type=F32)
         wout_grad = scatter_all(wout_part)
         dq, dkv = attn_backward(core_arr, qkv_seq, grad_attn_seq, attn_seq, lse, cos, sin)
-        dqkv_mine = jnp.concatenate([dq[:rows], dkv[:rows]], axis=1)
-        dqkv_other = swap(jnp.concatenate([dq[rows:], dkv[rows:]], axis=1))
-        dqkv = in_order(dqkv_mine, dqkv_other, 1)
-        qkv_part = lax.dot_general(normed_a, dqkv, tn, preferred_element_type=F32)
-        qkv_grad = scatter_all(qkv_part)
+        normed_a_full = jnp.concatenate([normed_a, swap(normed_a)], axis=0)
+        dqkv_seq = jnp.concatenate([dq, dkv], axis=1)
+        qkv_part = lax.dot_general(normed_a_full, dqkv_seq, tn, preferred_element_type=F32)
+        dqkv = in_order(dqkv_seq[:rows], swap(dqkv_seq[rows:]), 1)
+        qkv_rows = scatter_dp(qkv_part)
+        qkv_mine_rows = jnp.where(first, qkv_rows[:shard], qkv_rows[shard:])
+        qkv_grad = in_order(qkv_mine_rows, swap(jnp.where(first, qkv_rows[shard:], qkv_rows[:shard])), 1)
         grad_normed_a = dot_nt(dqkv, w_qkv).astype(BF16).astype(F32)
         grad_rows_a, gain1_grad = rms_backward(grad_normed_a, x_f, gain1)
         in_grad = (grad_hidden.astype(F32) + grad_rows_a).astype(BF16)
-        gain_grads = (scatter_all(gain1_grad), scatter_all(gain2_grad))
+        gain_sums = jnp.stack([gain1_grad, gain2_grad], axis=0)
+        gain_sums = gain_sums + swap(gain_sums)
+        bit = 1
+        while bit < n_dp:
+            gain_sums = gain_sums + lax.ppermute(gain_sums, "dp", [(d, d ^ bit) for d in range(n_dp)])
+            bit *= 2
+        me = lax.axis_index("dp") * (n_all // n_dp) + core
+        gain_grads = lax.dynamic_slice_in_dim(gain_sums, me * shard, shard, axis=1)
 
         def out_part(lo, hi):
             return sum(dot(mixed[k][lo:hi], w2[k]) for k in range(len(r_cuts)))

time: 1450 us -> 1880 us (1.30)
  waiting for transfers between devices: 54.3 us -> 570 us
  Pallas kernels: 603 us -> 531 us
  blocking collectives: 22.8 us -> 0 us
  local copies, waits for them, and re-layouts: 67.4 us -> 87.2 us
    reduce_scatter x4 -> x5, waiting for transfers between devices: 0.01 us -> 405 us  [scatter_dp(): return lax.psum_scatter(values, 'dp', scatter_dimension=0, tiled=True)]
    all_gather x4, waiting for transfers between devices: 0.04 us -> 109 us  [gather_dp(): return lax.all_gather(values, 'dp', axis=0, tiled=True)]
    pallas_call x1, Pallas kernels: 196 us -> 124 us  [attn_forward(): pl.pallas_call(attn_fwd_kernel, grid_spec=pltpu.PrefetchScalarGridSpec(nu...]
    reduce_scatter x2 -> x1, waiting for transfers between devices: 0.01 us -> 29.3 us  [scatter_all(): return lax.psum_scatter(values, flat_axes, scatter_dimension=0, tiled=True)]
    unnamed x1 -> x0, blocking collectives: 22.8 us -> none
  transfers between devices with their start and end apart: 25 -> 30, of which waited for: 8 -> 11; matrix products, arithmetic and copies ran while one was open for 51% -> 31% of each run, Pallas kernels for 42% -> 22%
where the time goes in v2:
time: 1880 us; the launch traced here: 1870 us
  waiting for transfers between devices  570 us (30%)
  matrix products  546 us (29%)
  Pallas kernels  531 us (28%)
  other arithmetic  115 us (6%)
  local copies, waits for them, and re-layouts  87.2 us (5%)
    reduce_scatter x5, waiting for transfers between devices, scatter_dp(): return lax.psum_scatter(values, 'dp', scatter_dimension=0, tiled=True)  405 us
    pallas_call x2, Pallas kernels, ffn_chunk(): pl.pallas_call(ffn_kernel, grid=(cols // FT, rows // bm), in_specs=[pl.Bl...  219 us
    dot_general x6, matrix products, dot_nt(): return lax.dot_general(a, b, NT, preferred_element_type=F32)  190 us
    pallas_call x1, Pallas kernels, attn_backward(): pl.pallas_call(attn_bwd_kernel, grid_spec=pltpu.PrefetchScalarGridSpec(nu...  167 us
    dot_general x2, matrix products, layer(): gu_k = lax.dot_general(normed_full, dgu_k, tn, preferred_element_type=F32)  138 us
    pallas_call x1, Pallas kernels, attn_forward(): pl.pallas_call(attn_fwd_kernel, grid_spec=pltpu.PrefetchScalarGridSpec(nu...  124 us
    all_gather x4, waiting for transfers between devices, gather_dp(): return lax.all_gather(values, 'dp', axis=0, tiled=True)  109 us
    dot_general x5, matrix products, dot(): return jnp.dot(a, b, preferred_element_type=F32)  107 us
  transfers between devices with their start and end apart: 30, of which 11 were waited for; matrix products, arithmetic and copies ran while one was open for 31% of the time, Pallas kernels for 22%

profile of v2, /device:TPU:0, one launch (start us, length us, event | category | flops | bytes accessed | tf_op | source)
XLA Modules:
  0.0 1872.2 jit_solution(4007147809870562602)
XLA Ops:
  44.5 7.9 fusion.61
  60.0 6.6 slice.553.w_ref
  66.6 20.6 %qkv_project.1 = (bf16[2048,2048]{1,0:T(8,128)(2,1)}, bf16[2048,1536]{1,0:T(8,128)(2,1)}) custom-call(bf16[2048,1536]{1,0:T(8,128)(2,1)} %bitcast.63, f32[1,1536]{1,0:T(1,128)} %reshape.98.g_ref, bf16[1536,2048]{1,0:T(8,128)(2,1)} %slice.553.w_ref, f32[4096,128]{1,0:T(8,128)} %get-tuple-element.170.cos_ref.cos_all_ref, ...), custom_call_target="tpu_custom_call" | custom-call | flops 12884901888 | bytes 27262976 | tf_op jit(solution)/shard_map/qkv_project/pallas_call | solution.py:57
  87.2 6.0 broadcast_select_fusion.1
  96.2 7.2 collective-permute-done.6
  106.1 7.7 pad_maximum_fusion.2.q_ref.k_ref.v_ref
  113.8 124.2 %attn_forward.1 = (bf16[4096,768]{1,0:T(8,128)(2,1)}, f32[8,8,512]{2,1,0:T(8,128)}) custom-call(s32[1]{0:T(128)} %bitcast.1.c_ref, bf16[4096,1024]{1,0:T(8,128)(2,1)} %pad_maximum_fusion.2.q_ref.k_ref.v_ref, bf16[4096,1024]{1,0:T(8,128)(2,1)} %pad_maximum_fusion.2.q_ref.k_ref.v_ref, bf16[4096,1024]{1,0:T(8,128)(2,1)} %pad_maximum_fusion.2.q_ref.k_ref.v_ref), custom_call_target="tpu_custom_call" | custom-call | flops 51539607552 | bytes 16777216 | tf_op jit(solution)/shard_map/attn_forward/pallas_call | solution.py:144
  237.9 5.9 fusion.85
  244.4 5.5 collective-permute-done.2
  249.9 15.7 fusion.30
  268.6 12.7 pad_maximum_fusion.1.dy_ref
  283.9 5.7 pad_maximum_fusion.w_ref
  289.6 94.5 %ffn_chunk.2 = (bf16[4096,1920]{1,0:T(8,128)(2,1)}, bf16[4096,3840]{1,0:T(8,128)(2,1)}) custom-call(bf16[4096,1536]{1,0:T(8,128)(2,1)} %pad_maximum_fusion.w_ref, bf16[4096,1536]{1,0:T(8,128)(2,1)} %pad_maximum_fusion.1.dy_ref, bf16[1536,3840]{1,0:T(8,128)(2,1)} %all-gather.11.cloned.1.call-done.w13_ref, bf16[1920,1536]{1,0:T(8,128)(2,1)} %all-gather.13.cloned.1.call-done.w2_ref), custom_call_target="tpu_custom_call" | custom-call | flops 72477573120 | bytes 115212288 | tf_op jit(solution)/shard_map/ffn_chunk/pallas_call | solution.py:309
  384.1 108.8 %all-gather.15.cloned.1.call-done.w13_ref = bf16[1536,5120]{1,0:T(8,128)(2,1)} async-done(((bf16[384,5120]{1,0:T(8,128)(2,1)}), bf16[1536,5120]{1,0:T(8,128)(2,1)}) %all-gather.15.cloned.1.call-update) | async-done | bytes 15728656 | tf_op jit(solution)/shard_map/all_gather | solution.py:349
  492.8 124.2 %ffn_chunk.3 = (bf16[4096,2560]{1,0:T(8,128)(2,1)}, bf16[4096,5120]{1,0:T(8,128)(2,1)}) custom-call(bf16[4096,1536]{1,0:T(8,128)(2,1)} %pad_maximum_fusion.w_ref, bf16[4096,1536]{1,0:T(8,128)(2,1)} %pad_maximum_fusion.1.dy_ref, bf16[1536,5120]{1,0:T(8,128)(2,1)} %all-gather.15.cloned.1.call-done.w13_ref, bf16[2560,1536]{1,0:T(8,128)(2,1)} %all-gather.17.cloned.1.call-done.w2_ref), custom_call_target="tpu_custom_call" | custom-call | flops 96636764160 | bytes 136839168 | tf_op jit(solution)/shard_map/ffn_chunk/pallas_call | solution.py:309
  617.0 41.9 %fusion = f32[2048,1536]{1,0:T(8,128)} fusion(bf16[1536,5120]{1,0:T(8,128)(2,1)} %all-gather.15.cloned.1.call-done.w13_ref, bf16[4096,5120]{1,0:T(8,128)(2,1)} %get-tuple-element.26), kind=kOutput, calls=%fused_computation | convolution fusion | flops 32212254720 | bytes 49283072 | tf_op jit(solution)/shard_map/dot_general | solution.py:26
  658.9 33.7 %fusion.43 = f32[2048,1536]{1,0:T(8,128)} fusion(f32[2048,1536]{1,0:T(8,128)} %fusion, bf16[1536,3840]{1,0:T(8,128)(2,1)} %all-gather.11.cloned.1.call-done.w13_ref, bf16[4096,3840]{1,0:T(8,128)(2,1)} %get-tuple-element.25), kind=kOutput, calls=%fused_computation.52 | convolution fusion | flops 24162336768 | bytes 52690944 | tf_op jit(solution)/shard_map/dot_general | solution.py:26
  692.6 41.9 %fusion.2 = f32[2048,1536]{1,0:T(8,128)} fusion(bf16[1536,5120]{1,0:T(8,128)(2,1)} %all-gather.15.cloned.1.call-done.w13_ref, bf16[4096,5120]{1,0:T(8,128)(2,1)} %get-tuple-element.26), kind=kOutput, calls=%fused_computation.2 | convolution fusion | flops 32212254720 | bytes 49283072 | tf_op jit(solution)/shard_map/dot_general | solution.py:26
  734.6 39.8 %fusion.29 = (f32[1536]{0:T(1024)}, f32[2048]{0:T(1024)S(1)}, bf16[2048,1536]{1,0:T(8,128)(2,1)}) fusion(bf16[2048,1536]{1,0:T(8,128)(2,1)} %copy-done.3, f32[2048]{0:T(1024)S(1)} %copy-done.18, f32[1536]{0:T(1024)S(1)} %copy-done.14, f32[2048,1536]{1,0:T(8,128)} %collective-permute-done.8, f32[2048,1536]{1,0:T(8,128)} %fusion.2, ...), kind=kOutput, calls=%fused_computation.37 | convolution fusion | flops 24193789952 | bytes 65302528 | tf_op jit(solution)/shard_map/dot_general | solution.py:26
  774.4 8.8 fusion.22
  783.2 11.1 convolution_convert_fusion
  795.4 5.3 collective-permute-done.9
  803.8 167.5 %attn_backward.1 = (bf16[4096,768]{1,0:T(8,128)(2,1)}, bf16[4096,256]{1,0:T(8,128)(2,1)}) custom-call(s32[1]{0:T(128)} %bitcast.1.c_ref, bf16[4096,1024]{1,0:T(8,128)(2,1)} %pad_maximum_fusion.2.q_ref.k_ref.v_ref, bf16[4096,768]{1,0:T(8,128)(2,1)} %pad_maximum_fusion.4.do_ref, bf16[4096,768]{1,0:T(8,128)(2,1)} %get-tuple-element.22.o_ref, ...), custom_call_target="tpu_custom_call" | custom-call | flops 128849018880 | bytes 33554432 | tf_op jit(solution)/shard_map/attn_backward/pallas_call | solution.py:257
  971.3 3.8 constant_dynamic-update-slice_fusion.1
  978.6 17.1 fusion.33
  995.8 61.8 %fusion.83 = f32[1536,3840]{1,0:T(8,128)} fusion(bf16[4096,3840]{1,0:T(8,128)(2,1)} %get-tuple-element.25, bf16[2048,1536]{1,0:T(8,128)(2,1)} %copy-done.6, bf16[2048,1536]{1,0:T(8,128)(2,1)} %copy-done.4), kind=kOutput, calls=%fused_computation.181 | convolution fusion | flops 48343547904 | bytes 67633152 | tf_op jit(solution)/shard_map/dot_general | solution.py:445
  1057.6 76.7 %fusion.82 = f32[1536,5120]{1,0:T(8,128)} fusion(bf16[4096,5120]{1,0:T(8,128)(2,1)} %get-tuple-element.26, bf16[2048,1536]{1,0:T(8,128)(2,1)} %copy-done.6, bf16[2048,1536]{1,0:T(8,128)(2,1)} %copy-done.4), kind=kOutput, calls=%fused_computation.180 | convolution fusion | flops 64449675264 | bytes 85983232 | tf_op jit(solution)/shard_map/dot_general | solution.py:445
  1134.4 34.4 %fusion.81 = f32[1920,1536]{1,0:T(8,128)} fusion(bf16[4096,1920]{1,0:T(8,128)(2,1)} %get-tuple-element.23, bf16[2048,1536]{1,0:T(8,128)(2,1)} %collective-permute-done.4, bf16[2048,1536]{1,0:T(8,128)(2,1)} %bitcast.66), kind=kOutput, calls=%fused_computation.179 | convolution fusion | flops 24184356864 | bytes 40108032 | tf_op jit(solution)/shard_map/dot_general | solution.py:444
  1168.9 42.4 %fusion.80 = f32[2560,1536]{1,0:T(8,128)} fusion(bf16[4096,2560]{1,0:T(8,128)(2,1)} %get-tuple-element.24, bf16[2048,1536]{1,0:T(8,128)(2,1)} %collective-permute-done.4, bf16[2048,1536]{1,0:T(8,128)(2,1)} %bitcast.67), kind=kOutput, calls=%fused_computation.178 | convolution fusion | flops 32237420544 | bytes 49283072 | tf_op jit(solution)/shard_map/dot_general | solution.py:444
  1211.3 23.2 %fusion.37 = f32[2048,1536]{1,0:T(8,128)} fusion(bf16[2560,1536]{1,0:T(8,128)(2,1)} %all-gather.17.cloned.1.call-done.w2_ref, bf16[4096,2560]{1,0:T(8,128)(2,1)} %get-tuple-element.24), kind=kOutput, calls=%fused_computation.48 | convolution fusion | flops 16106127360 | bytes 30932992 | tf_op jit(solution)/shard_map/dot_general | solution.py:22
  1234.5 22.4 %convolution_add_fusion = f32[2048,1536]{1,0:T(8,128)} fusion(f32[2048,1536]{1,0:T(8,128)} %fusion.37, bf16[1920,1536]{1,0:T(8,128)(2,1)} %all-gather.13.cloned.1.call-done.w2_ref, bf16[4096,1920]{1,0:T(8,128)(2,1)} %get-tuple-element.23), kind=kOutput, calls=%fused_computation.53 | convolution fusion | flops 12082741248 | bytes 38928384 | tf_op jit(solution)/shard_map/dot_general | solution.py:22
  1256.9 4.3 fusion.26
  1261.3 6.7 fusion.84
  1268.5 20.5 %fusion.39 = f32[2048,1536]{1,0:T(8,128)} fusion(bf16[2560,1536]{1,0:T(8,128)(2,1)S(1)} %bitcast.75, bf16[4096,2560]{1,0:T(8,128)(2,1)} %get-tuple-element.24), kind=kOutput, calls=%fused_computation.50 | convolution fusion | flops 16106127360 | bytes 30932992 | tf_op jit(solution)/shard_map/dot_general | solution.py:22
  1289.1 17.1 fusion.60
  1306.9 21.5 %fusion.24 = (f32[1536]{0:T(1024)S(1)}, f32[2048]{0:T(1024)S(1)}, bf16[2048,1536]{1,0:T(8,128)(2,1)}) fusion(f32[2048]{0:T(1024)S(1)} %add_rsqrt_fusion, bf16[1,2048,1536]{2,1,0:T(8,128)(2,1)} %param.12, f32[1536]{0:T(1024)S(1)} %copy-done.16, bf16[1536,2176]{1,0:T(8,128)(2,1)} %all-gather.7.cloned.1.call-done, ...), kind=kOutput, calls=%fused_computation.32 | convolution fusion | flops 12950958080 | bytes 27291648 | tf_op jit(solution)/shard_map/dot_general | solution.py:26
  1328.6 25.0 %fusion.56 = bf16[1,2048,1536]{2,1,0:T(8,128)(2,1)} fusion(f32[2048,1536]{1,0:T(8,128)} %collective-permute-done.7, f32[2048,1536]{1,0:T(8,128)} %fusion.39, bf16[1920,1536]{1,0:T(8,128)(2,1)S(1)} %bitcast.77, bf16[4096,1920]{1,0:T(8,128)(2,1)} %get-tuple-element.23, bf16[2048,1536]{1,0:T(8,128)(2,1)} %copy-done.3), kind=kOutput, calls=%fused_computation.68 | convolution fusion | flops 12095324160 | bytes 51511296 | tf_op jit(solution)/shard_map/dot_general | solution.py:22
  1360.7 12.3 fusion.59
  1373.8 4.6 slice_select_fusion.2
  1378.8 158.6 %reduce-scatter.13.cloned.1.call-done = f32[384,5120]{1,0:T(8,128)} async-done(((f32[1536,5120]{1,0:T(8,128)}), f32[384,5120]{1,0:T(8,128)}) %reduce-scatter.13.cloned.1.call-update) | async-done | bytes 7864336 | tf_op jit(solution)/shard_map/reduce_scatter | solution.py:355
  1537.4 5.8 slice_select_fusion
  1545.9 103.0 %reduce-scatter.15.cloned.1.call-done = f32[480,1536]{1,0:T(8,128)} async-done(((f32[1920,1536]{1,0:T(8,128)}), f32[480,1536]{1,0:T(8,128)}) %reduce-scatter.15.cloned.1.call-update) | async-done | bytes 2949136 | tf_op jit(solution)/shard_map/reduce_scatter | solution.py:355
  1648.9 143.8 %reduce-scatter.17.cloned.1.call-done = f32[640,1536]{1,0:T(8,128)} async-done(((f32[2560,1536]{1,0:T(8,128)}), f32[640,1536]{1,0:T(8,128)}) %reduce-scatter.17.cloned.1.call-update) | async-done | bytes 3932176 | tf_op jit(solution)/shard_map/reduce_scatter | solution.py:355
  1792.8 6.4 pad_maximum_fusion.3
  1799.2 5.1 broadcast_select_fusion.8
  1818.8 8.8 concatenate.200
  1827.5 8.3 concatenate.205
  1835.8 29.3 %reduce-scatter.9.cloned.1.call-done = f32[192,1536]{1,0:T(8,128)} async-done(((f32[1536,1536]{1,0:T(8,128)}), f32[192,1536]{1,0:T(8,128)}) %reduce-scatter.9.cloned.1.call-update) | async-done | bytes 1179664 | tf_op jit(solution)/shard_map/reduce_scatter | solution.py:358
  (209 shorter events, 91.2 us)
Async XLA Ops:
  7.2 50.6 %all-gather.7.cloned.1.call-start = ((), (), s32[]{:S(2)}) async-start(), calls=%async_computation.6 | async-start | bytes 7520256 | tf_op jit(solution)/shard_map/all_gather | solution.py:352
  13.3 231.1 %all-gather.9.cloned.1.call-start = ((), (), s32[]{:S(2)}) async-start(), calls=%async_computation.7 | async-start | bytes 5308416 | tf_op jit(solution)/shard_map/all_gather | solution.py:352
  14.1 275.5 %all-gather.13.cloned.1.call-start = ((), (), s32[]{:S(2)}) async-start(), calls=%async_computation.9 | async-start | bytes 7372800 | tf_op jit(solution)/shard_map/all_gather | solution.py:349
  16.8 272.8 %all-gather.11.cloned.1.call-start = ((), (), s32[]{:S(2)}) async-start(), calls=%async_computation.8 | async-start | bytes 14745600 | tf_op jit(solution)/shard_map/all_gather | solution.py:349
  23.2 3.8 collective-permute-start.5
  28.9 355.1 %all-gather.17.cloned.1.call-start = ((), (), s32[]{:S(2)}) async-start(), calls=%async_computation.11 | async-start | bytes 9830400 | tf_op jit(solution)/shard_map/all_gather | solution.py:349
  31.9 460.9 %all-gather.15.cloned.1.call-start = ((), (), s32[]{:S(2)}) async-start(), calls=%async_computation.10 | async-start | bytes 19660800 | tf_op jit(solution)/shard_map/all_gather | solution.py:349
  32.0 12.5 collective-permute-start
  59.3 7.2 copy-start.15
  59.4 206.3 %copy-start.13 = (f32[1536]{0:T(1024)}, f32[1536]{0:T(1024)S(1)}, u32[]{:S(2)}) copy-start(f32[1536]{0:T(1024)S(1)} %get-tuple-element.57) | copy-start | bytes 18436
  87.2 8.2 copy-start.9
  93.2 12.9 collective-permute-start.1
  96.0 7.4 collective-permute-start.6
  106.0 1253.1 %reduce-scatter.7.cloned.1.call-start = ((), (), s32[]{:S(2)}) async-start(), calls=%async_computation.12 | async-start | bytes 7864320 | tf_op jit(solution)/shard_map/reduce_scatter | solution.py:355
  243.9 6.0 collective-permute-start.2
  244.2 24.4 %collective-permute-start.4 = (bf16[2048,1536]{1,0:T(8,128)(2,1)}, bf16[2048,1536]{1,0:T(8,128)(2,1)}, u32[]{:S(2)}, u32[]{:S(2)}) collective-permute-start(bf16[2048,1536]{1,0:T(8,128)(2,1)} %bitcast.64), channel_id=1, source_target_pairs={{0,1},{1,0},{2,3},{3,2},{4,5},{5,4},{6,7},{7,6}} | collective-permute-start | bytes 18874376 | tf_op jit(solution)/shard_map/ppermute | solution.py:346
  268.3 13.0 copy-start.4
  268.3 13.0 collective-permute-start.3
  692.6 41.9 %copy-start.14 = (f32[1536]{0:T(1024)S(1)}, f32[1536]{0:T(1024)}, u32[]{:S(2)}) copy-start(f32[1536]{0:T(1024)} %copy-done.13) | copy-start | bytes 18436
  692.6 41.9 %copy-start.18 = (f32[2048]{0:T(1024)S(1)}, f32[2048]{0:T(1024)}, u32[]{:S(2)}) copy-start(f32[2048]{0:T(1024)} %copy-done.17) | copy-start | bytes 24580
  692.6 41.9 %collective-permute-start.8 = (f32[2048,1536]{1,0:T(8,128)}, f32[2048,1536]{1,0:T(8,128)}, u32[]{:S(2)}, u32[]{:S(2)}) collective-permute-start(f32[2048,1536]{1,0:T(8,128)} %fusion.43), channel_id=1, source_target_pairs={{0,1},{1,0},{2,3},{3,2},{4,5},{5,4},{6,7},{7,6}} | collective-permute-start | bytes 37748744 | tf_op jit(solution)/shard_map/ppermute | solution.py:346
  774.4 8.8 copy-start.21
  783.2 11.1 copy-start.5
  794.9 5.8 collective-permute-start.9
  795.4 180.0 %collective-permute-start.14 = (bf16[2048,1536]{1,0:T(8,128)(2,1)}, bf16[2048,1536]{1,0:T(8,128)(2,1)}, u32[]{:S(2)}, u32[]{:S(2)}) collective-permute-start(bf16[2048,1536]{1,0:T(8,128)(2,1)} %get-tuple-element.30), channel_id=1, source_target_pairs={{0,1},{1,0},{2,3},{3,2},{4,5},{5,4},{6,7},{7,6}} | collective-permute-start | bytes 18874376 | tf_op jit(solution)/shard_map/ppermute | solution.py:346
  995.7 378.1 %reduce-scatter.11.cloned.1.call-start = ((), (), s32[]{:S(2)}) async-start(), calls=%async_computation.14 | async-start | bytes 29491200 | tf_op jit(solution)/shard_map/reduce_scatter | solution.py:355
  1057.6 479.8 %reduce-scatter.13.cloned.1.call-start = ((), (), s32[]{:S(2)}) async-start(), calls=%async_computation.15 | async-start | bytes 39321600 | tf_op jit(solution)/shard_map/reduce_scatter | solution.py:355
  1134.3 514.6 %reduce-scatter.15.cloned.1.call-start = ((), (), s32[]{:S(2)}) async-start(), calls=%async_computation.16 | async-start | bytes 14745600 | tf_op jit(solution)/shard_map/reduce_scatter | solution.py:355
  1168.8 623.9 %reduce-scatter.17.cloned.1.call-start = ((), (), s32[]{:S(2)}) async-start(), calls=%async_computation.17 | async-start | bytes 19660800 | tf_op jit(solution)/shard_map/reduce_scatter | solution.py:355
  1211.3 653.9 %reduce-scatter.9.cloned.1.call-start = ((), (), s32[]{:S(2)}) async-start(), calls=%async_computation.13 | async-start | bytes 10616832 | tf_op jit(solution)/shard_map/reduce_scatter | solution.py:358
  1256.9 71.6 %collective-permute-start.7 = (f32[2048,1536]{1,0:T(8,128)}, f32[2048,1536]{1,0:T(8,128)}, u32[]{:S(2)}, u32[]{:S(2)}) collective-permute-start(f32[2048,1536]{1,0:T(8,128)} %convolution_add_fusion), channel_id=1, source_target_pairs={{0,1},{1,0},{2,3},{3,2},{4,5},{5,4},{6,7},{7,6}} | collective-permute-start | bytes 37748744 | tf_op jit(solution)/shard_map/ppermute | solution.py:346
  1256.9 11.6 slice-start.4
  1268.0 21.1 %slice-start.2 = ((s8[6291456]{0:T(1024)(128)(4,1)}), s8[4194304]{0:T(1024)(128)(4,1)S(1)}, s32[]{:S(2)}) async-start(s8[6291456]{0:T(1024)(128)(4,1)} %bitcast.68), calls=%async_computation.20 | async-start | bytes 8388608
  1268.0 21.1 %copy-start.19 = (f32[1536]{0:T(1024)S(1)}, f32[1536]{0:T(1024)}, u32[]{:S(2)}) copy-start(f32[1536]{0:T(1024)} %get-tuple-element.55) | copy-start | bytes 18436
  1268.0 21.1 %slice-start.3 = ((s8[6291456]{0:T(1024)(128)(4,1)}), s8[2097152]{0:T(1024)(128)(4,1)S(1)}, s32[]{:S(2)}) async-start(s8[6291456]{0:T(1024)(128)(4,1)} %bitcast.68), calls=%async_computation.21 | async-start | bytes 4194304
  1268.0 21.1 %copy-start.7 = (bf16[2048,768]{1,0:T(8,128)(2,1)S(1)}, bf16[2048,768]{1,0:T(8,128)(2,1)}, u32[]{:S(2)}) copy-start(bf16[2048,768]{1,0:T(8,128)(2,1)} %get-tuple-element.69) | copy-start | bytes 9437188
  1268.0 38.2 %collective-permute-start.10 = (bf16[2048,1024]{1,0:T(8,128)(2,1)}, bf16[2048,1024]{1,0:T(8,128)(2,1)}, u32[]{:S(2)}, u32[]{:S(2)}) collective-permute-start(bf16[2048,1024]{1,0:T(8,128)(2,1)} %get-tuple-element.64), channel_id=1, source_target_pairs={{0,1},{1,0},{2,3},{3,2},{4,5},{5,4},{6,7},{7,6}} | collective-permute-start | bytes 12582920 | tf_op jit(solution)/shard_map/ppermute | solution.py:346
  1306.2 22.4 %slice-start.6 = ((s8[5898240]{0:T(1024)(128)(4,1)}), s8[1703936]{0:T(1024)(128)(4,1)S(1)}, s32[]{:S(2)}) async-start(s8[5898240]{0:T(1024)(128)(4,1)} %bitcast.76), calls=%async_computation.24 | async-start | bytes 3407872
  1306.9 21.7 %slice-start.7 = ((s8[5898240]{0:T(1024)(128)(4,1)}), s8[4194304]{0:T(1024)(128)(4,1)S(1)}, s32[]{:S(2)}) async-start(s8[5898240]{0:T(1024)(128)(4,1)} %bitcast.76), calls=%async_computation.25 | async-start | bytes 8388608
  1328.4 25.2 %collective-permute-start.11 = (f32[2,1536]{1,0:T(2,128)S(1)}, f32[2,1536]{1,0:T(2,128)S(1)}, u32[]{:S(2)}, u32[]{:S(2)}) collective-permute-start(f32[2,1536]{1,0:T(2,128)S(1)} %pad_maximum_fusion.29), channel_id=1, source_target_pairs={{0,1},{1,0},{2,3},{3,2},{4,5},{5,4},{6,7},{7,6}} | collective-permute-start | bytes 36872 | tf_op jit(solution)/shard_map/ppermute | solution.py:346
  1353.6 4.1 collective-permute-start.12
  1357.7 15.3 collective-permute-start.13
  1360.7 12.9 collective-permute-start.15
  1378.5 420.7 %collective-permute-start.16 = (f32[192,3840]{1,0:T(8,128)}, f32[192,3840]{1,0:T(8,128)}, u32[]{:S(2)}, u32[]{:S(2)}) collective-permute-start(f32[192,3840]{1,0:T(8,128)} %slice_select_fusion.2), channel_id=1, source_target_pairs={{0,1},{1,0},{2,3},{3,2},{4,5},{5,4},{6,7},{7,6}} | collective-permute-start | bytes 8847368 | tf_op jit(solution)/shard_map/ppermute | solution.py:346
  1543.1 269.2 %collective-permute-start.17 = (f32[192,5120]{1,0:T(8,128)}, f32[192,5120]{1,0:T(8,128)}, u32[]{:S(2)}, u32[]{:S(2)}) collective-permute-start(f32[192,5120]{1,0:T(8,128)} %slice_select_fusion), channel_id=1, source_target_pairs={{0,1},{1,0},{2,3},{3,2},{4,5},{5,4},{6,7},{7,6}} | collective-permute-start | bytes 11796488 | tf_op jit(solution)/shard_map/ppermute | solution.py:346
  1818.8 8.8 copy-start.11
  1818.8 8.8 copy-start.12
  1827.5 37.6 %copy-start.1 = (bf16[192,12,128]{2,0,1:T(8,128)(2,1)S(1)}, bf16[192,12,128]{2,0,1:T(8,128)(2,1)}, u32[]{:S(2)}) copy-start(bf16[192,12,128]{2,0,1:T(8,128)(2,1)} %param.17) | copy-start | bytes 1769476
  (12 other events, 43.5 us)
Sparse Core Ops, SparseCore 0:
  13.4 44.2 all-gather.6
  59.6 33.2 all-gather.8
  94.6 61.1 all-gather.12
  158.0 110.2 all-gather.10
  270.0 77.5 all-gather.16
  349.8 142.9 all-gather.14
  995.9 64.4 reduce-scatter.6
  1063.4 203.4 reduce-scatter.10
  1269.9 267.4 reduce-scatter.12
  1540.3 108.5 reduce-scatter.14
  1652.0 140.7 reduce-scatter.16
  1796.6 68.4 reduce-scatter.8
